TPU v7x, 256 devices: a 4x2x16 block of a 4x16x16 slice. The times are simulated.
256 devices in a mesh: grp: 2 (over y), seq: 64 (over z, x), head: 2 (over core).
Axes of the slice: x: 4, y: 2, z: 16, core: 2. Of those that a mesh axis runs over, the one named last changes fastest.
The devices are a block of a 4x16x16 slice.
Arguments:
- queries: bfloat16 [1024, 2, 128], P(('grp', 'seq'), 'head'), parts along dimension 0, may hold values from -6 to 6
- keys: bfloat16 [1024, 512, 8, 128], P(('grp', 'seq'), None, 'head'), parts along dimension 0, may hold values from -28 to 28
- values: bfloat16 [1024, 512, 8, 128], P(('grp', 'seq'), None, 'head'), parts along dimension 0, may hold values from -6 to 6
- lengths: int32 [32], P('grp'), parts along dimension 0, may hold values from 1 to 16384, 163840 in all
- slot_block: int32 [1024], P(('grp', 'seq')), parts along dimension 0, may hold values from 0 to 511, each once
Outputs:
- attended: bfloat16 [1024, 2, 128], P(('grp', 'seq'), 'head'), parts along dimension 0
There are 2 independent parts, one for each index of `grp`. A program takes and returns all parts, laid end to end along the dimension named above; each array names one. Nothing has to cross between parts.
Inputs may be any that keep to these rules, and one draw needn't show every extreme that they name: `slot_block`: each slot holds a different logical block; every block of every sequence has a slot. `lengths`: every sequence has at least one token.
All inputs are finite; a program needn't handle non-finite values.
Results may differ from a plain program's by a relative error of at most 0.0055.
Values may be sent and summed in bfloat16 or wider, within the bound.
A program may use at most 64 MiB of HBM per device.

v0:
```python
import math

import jax
import jax.numpy as jnp
from jax import lax
from jax.sharding import PartitionSpec as P


def from_everyone(array, axis):
    copies = jnp.broadcast_to(array, (lax.axis_size(axis), *array.shape))
    return lax.all_to_all(copies, axis, split_axis=0, concat_axis=0, tiled=True)


def in_order(tiles, dim):
    lengths = list(tiles.shape[1:])
    lengths[dim] *= tiles.shape[0]
    return jnp.moveaxis(tiles, 0, dim).reshape(lengths)


def gathered_copies(array, axis, dim):
    tiles = from_everyone(array, axis)
    return in_order(tiles, dim)


def taken_together(array, axis):
    return from_everyone(array, axis).max(axis=0)


def cut_along(array, dim, length):
    lengths = array.shape
    tiles = array.reshape(*lengths[:dim], length, lengths[dim] // length, *lengths[dim + 1 :])
    return jnp.moveaxis(tiles, dim, 0)


def summed_on_arrival(array, axis, dim):
    length = lax.axis_size(axis)
    tiles = lax.all_to_all(cut_along(array, dim, length), axis, 0, 0, tiled=True)
    return jnp.sum(tiles, axis=0)


def sent_together(arrays, axis, dim, along):
    widths = [math.prod(a.shape[along:]) for a in arrays]
    both = jnp.concatenate(
        [a.reshape(*a.shape[:along], w) for a, w in zip(arrays, widths)], axis=along
    )
    out = summed_on_arrival(both, axis, dim)
    tiles = jnp.split(out, [sum(widths[:k]) for k in range(1, len(widths))], axis=along)
    return tuple((b.reshape(*out.shape[:along], *a.shape[along:]) for a, b in zip(arrays, tiles)))


def slot_partial(q_one, key_one, val_one, live_one, factor):
    scores = jnp.einsum("kgd,tkd->kgt", q_one, key_one, preferred_element_type=jnp.float32) * factor
    live_row = live_one[None, None, :]
    peak = jnp.max(jnp.where(live_row, scores, -1e30), axis=-1)
    weights = jnp.where(live_row, jnp.exp(scores - peak[..., None]), 0.0).astype(jnp.bfloat16)
    total = jnp.sum(weights.astype(jnp.float32), axis=-1)
    partial_out = jnp.einsum("kgt,tkd->kgd", weights, val_one, preferred_element_type=jnp.float32)
    return (peak, total, partial_out)


def body(queries, keys, values, lengths, slot_block):
    rows = gathered_copies(queries, "seq", 0)
    slots, block, kv_local, head_dim = keys.shape
    batch = lengths.shape[0]
    group = rows.shape[0] // batch // kv_local
    factor = head_dim ** (-0.5)
    q_grouped = rows.reshape(batch, kv_local, group, head_dim)
    per_seq = slots * lax.axis_size("seq") // batch
    seq_of = slot_block // per_seq
    blk_of = slot_block % per_seq
    q_slot = jnp.take(q_grouped, seq_of, axis=0)
    positions = blk_of[:, None] * block + jnp.arange(block, dtype=jnp.int32)[None, :]
    live = positions < jnp.take(lengths, seq_of)[:, None]

    def run_slot(q_one, key_one, val_one, live_one):
        return slot_partial(q_one, key_one, val_one, live_one, factor)

    peaks, totals, partials = jax.vmap(run_slot)(q_slot, keys, values, live)
    member = seq_of[:, None] == jnp.arange(batch, dtype=jnp.int32)[None, :]
    best = jnp.max(jnp.where(member[:, :, None, None], peaks[:, None], -1e30), axis=0)
    scaled = jnp.exp(peaks - jnp.take(best, seq_of, axis=0))
    onehot = member.astype(jnp.float32)
    denom = jnp.einsum("sb,skg->bkg", onehot, scaled * totals, precision=lax.Precision.HIGHEST)
    numer = jnp.einsum(
        "sb,skgd->bkgd", onehot, scaled[..., None] * partials, precision=lax.Precision.HIGHEST
    )
    row_count = rows.shape[0]
    share = row_count // lax.axis_size("seq")
    top_peak = taken_together(best, "seq")
    rescale = jnp.exp(best - top_peak)
    own_total, own_out = sent_together(
        (
            (denom * rescale).reshape(row_count),
            (numer * rescale[..., None]).reshape(row_count, head_dim),
        ),
        "seq",
        0,
        1,
    )
    result = own_out / own_total[:, None]
    return result.astype(jnp.bfloat16).reshape(share, 1, head_dim)


def solution(mesh):
    placed = (
        P(("grp", "seq"), "head", None),
        P(("grp", "seq"), None, "head", None),
        P(("grp", "seq"), None, "head", None),
        P("grp"),
        P(("grp", "seq")),
    )
    return jax.shard_map(
        body, mesh=mesh, in_specs=placed, out_specs=P(("grp", "seq"), "head", None), check_vma=False
    )
```

profile of v0, /device:TPU:40, one launch (start us, length us, event | category | flops | bytes accessed | tf_op | source)
XLA Modules:
  0.0 113.5 jit_solution(9988716629397182596)
XLA Ops:
  0.0 0.0 copy-start
  0.0 1.3 %broadcast_in_dim.82 = bf16[64,8,1,128]{3,1,2,0:T(8,128)(2,1)} broadcast(bf16[8,128]{1,0:T(8,128)(2,1)} %bitcast.25), dimensions={1,3} | broadcast | bytes 133120 | tf_op jit(solution)/shard_map/broadcast_in_dim | solution.py:10
  1.4 29.0 %all-to-all-start = ((bf16[64,8,1,128]{3,1,2,0:T(8,128)(2,1)}), bf16[64,8,1,128]{3,1,2,0:T(8,128)(2,1)S(1)}, u32[]{:S(2)}, u32[]{:S(2)}) async-start(bf16[64,8,1,128]{3,1,2,0:T(8,128)(2,1)} %broadcast_in_dim.82), calls=%async_computation | async-start | bytes 262144 | tf_op jit(solution)/shard_map/all_to_all | solution.py:11
  30.4 0.7 compare_select_fusion
  31.1 0.1 iota_compare_fusion
  31.1 0.0 copy-done
  31.2 0.6 gather_fusion
  31.8 0.1 add_compare_fusion
  31.9 14.8 %all-to-all-done = bf16[64,8,1,128]{3,1,2,0:T(8,128)(2,1)S(1)} async-done(((bf16[64,8,1,128]{3,1,2,0:T(8,128)(2,1)}), bf16[64,8,1,128]{3,1,2,0:T(8,128)(2,1)S(1)}, u32[]{:S(2)}, u32[]{:S(2)}) %all-to-all-start) | async-done | bytes 131104 | tf_op jit(solution)/shard_map/all_to_all | solution.py:11
  46.7 0.6 gather_fusion.1
  47.3 3.5 %select_reduce_fusion = (f32[8,4,8]{2,1,0:T(4,128)S(1)}, f32[8,4,8,512]{3,2,1,0:T(8,128)S(1)}) fusion(pred[8,512]{1,0:T(8,128)(4,1)S(1)} %add_compare_fusion, bf16[8,512,4,128]{3,2,1,0:T(4,128)(2,1)} %param.6, bf16[8,4,8,128]{3,2,1,0:T(8,128)(2,1)S(1)} %gather_fusion.1, pred[8]{0:T(512)(128)(4,1)S(1)} %get-tuple-element.8), kind=kOutput, calls=%fused_computation.15 | convolution fusion | flops 33980160 | bytes 4789256 | tf_op jit(solution)/shard_map/vmap(kgd,tkd->kgt)/dot_general | solution.py:52
  50.8 0.1 select_reduce_fusion.1
  50.9 0.1 copy.27
  51.0 0.1 broadcast_bitcast_fusion
  51.1 0.3 convert_reduce_fusion
  51.4 0.6 gather_fusion.2
  51.9 1.0 reshape.116
  53.0 6.5 %all-to-all-start.1 = ((f32[64,1,512]{2,1,0:T(1,128)}), f32[64,1,512]{2,1,0:T(1,128)S(1)}, u32[]{:S(2)}, u32[]{:S(2)}) async-start(f32[64,1,512]{2,1,0:T(1,128)} %reshape.116), calls=%async_computation.1 | async-start | bytes 262144 | tf_op jit(solution)/shard_map/all_to_all | solution.py:11
  59.5 0.1 fusion.24
  59.5 0.1 copy.28
  59.6 2.9 %fusion.7 = f32[8,4,8,128]{3,2,1,0:T(8,128)S(1)} fusion(bf16[8,512,4,128]{3,2,1,0:T(4,128)(2,1)} %param.7, f32[8,4,8]{2,1,0:T(4,128)S(1)} %get-tuple-element.6, f32[8,4,8,512]{3,2,1,0:T(8,128)S(1)} %get-tuple-element.13, f32[8,4,8]{2,1,0:T(4,128)S(1)} %get-tuple-element.12, pred[8,512]{1,0:T(8,128)(4,1)S(1)} %add_compare_fusion), kind=kOutput, calls=%fused_computation.9 | convolution fusion | flops 33980416 | bytes 4855808 | tf_op jit(solution)/shard_map/vmap(kgt,tkd->kgd)/dot_general | solution.py:57
  62.5 11.9 %all-to-all-done.1 = f32[64,1,512]{2,1,0:T(1,128)S(1)} async-done(((f32[64,1,512]{2,1,0:T(1,128)}), f32[64,1,512]{2,1,0:T(1,128)S(1)}, u32[]{:S(2)}, u32[]{:S(2)}) %all-to-all-start.1) | async-done | bytes 131104 | tf_op jit(solution)/shard_map/all_to_all | solution.py:11
  74.4 0.5 broadcast.123
  74.9 1.0 reduce.2
  75.9 0.4 reshape.117
  76.2 0.1 bitcast_reduce_fusion
  76.4 0.4 convolution_multiply_fusion
  76.7 0.1 copy.32
  76.8 0.2 fusion.10
  77.0 0.1 copy.29
  77.1 0.4 copy.33
  77.6 0.2 pad_maximum_fusion
  77.8 34.9 %all_to_all.15 = f32[64,8,129]{2,1,0:T(8,128)S(1)} all-to-all(f32[64,8,129]{2,1,0:T(8,128)S(1)} %pad_maximum_fusion), channel_id=1, replica_groups=mesh['grp'=2,'seq'=64,'head'=2] {'seq'}, dimensions={0} | all-to-all | bytes 528384 | tf_op jit(solution)/shard_map/all_to_all | solution.py:37
  112.7 0.1 reduce_sum.19
  112.7 0.1 slice_reduce_fusion
  112.9 0.7 fusion.20
  (3 shorter events, 0.0 us)
Async XLA Ops:
  0.0 31.1 %copy-start = (s32[16]{0:T(128)S(1)}, s32[16]{0:T(128)}, u32[]{:S(2)}) copy-start(s32[16]{0:T(128)} %param.8) | copy-start | bytes 196
  1.4 45.4 %all-to-all-start = ((bf16[64,8,1,128]{3,1,2,0:T(8,128)(2,1)}), bf16[64,8,1,128]{3,1,2,0:T(8,128)(2,1)S(1)}, u32[]{:S(2)}, u32[]{:S(2)}) async-start(bf16[64,8,1,128]{3,1,2,0:T(8,128)(2,1)} %broadcast_in_dim.82), calls=%async_computation | async-start | bytes 262144 | tf_op jit(solution)/shard_map/all_to_all | solution.py:11
  53.0 21.4 %all-to-all-start.1 = ((f32[64,1,512]{2,1,0:T(1,128)}), f32[64,1,512]{2,1,0:T(1,128)S(1)}, u32[]{:S(2)}, u32[]{:S(2)}) async-start(f32[64,1,512]{2,1,0:T(1,128)} %reshape.116), calls=%async_computation.1 | async-start | bytes 262144 | tf_op jit(solution)/shard_map/all_to_all | solution.py:11
where the time goes:
time: 114 us
  starting transfers between devices  35.5 us (31%)
  blocking collectives  34.9 us (31%)
  waiting for transfers between devices  26.7 us (23%)
  matrix products  6.98 us (6%)
  local copies, waits for them, and re-layouts  6.04 us (5%)
  other arithmetic  3.3 us (3%)
    all_to_all x2, starting transfers between devices, from_everyone(): return lax.all_to_all(copies, axis, split_axis=0, concat_axis=0, tiled=True)  35.5 us
    all_to_all x1, blocking collectives, summed_on_arrival(): lax.all_to_all(cut_along(array, dim, length), axis, 0, 0, tiled=True)  34.9 us
    all_to_all x2, waiting for transfers between devices, from_everyone(): return lax.all_to_all(copies, axis, split_axis=0, concat_axis=0, tiled=True)  26.7 us
    dot_general x1, matrix products, slot_partial(): jnp.einsum('kgd,tkd->kgt', q_one, key_one, preferred_element_type=jnp.flo...  3.51 us
    dot_general x1, matrix products, slot_partial(): jnp.einsum('kgt,tkd->kgd', weights, val_one, preferred_element_type=jnp.f...  2.91 us
  transfers between devices with their start and end apart: 2, of which 2 were waited for; matrix products, arithmetic and copies ran while one was open for 4% of the time, Pallas kernels for 0%

commit v1 on v0

v1 whole, which is shorter than its diff:
```python
import functools
import math

import jax
import jax.numpy as jnp
from jax import lax
from jax.experimental import pallas as pl
from jax.experimental.pallas import tpu as pltpu
from jax.sharding import PartitionSpec as P

MESH = pl.DeviceIdType.MESH
F32 = jnp.float32
BF16 = jnp.bfloat16
NEG = -1e30


def by_distance(count):
    return sorted(range(1, count), key=lambda d: -min(d, count - d)) + [0]


def attend(dims, q_hbm, k_hbm, v_hbm, len_hbm, slot_hbm, o_ref,
           kbuf, vbuf, ktr, q_own, q_all, q_stage, lens, slot, out_send, out_recv, st_send, st_recv,
           ksem, vsem, small_sem, q_send_sem, q_recv_sem, o_send_sem, o_recv_sem, s_send_sem, s_recv_sem):
    nz, nx, slots, block, group, hd = dims
    n = nz * nx
    half = 2
    pairs = nx // half
    rows = half * group
    wide = block * half
    me = lax.axis_index("seq")
    mz, mx = me // nx, lax.rem(me, nx)

    barrier = pltpu.get_barrier_semaphore()
    offsets = [(dz, dx) for dz in by_distance(nz) for dx in by_distance(nx) if dz or dx]
    where = [(lax.rem(mz + dz, nz), lax.rem(mx + dx, nx)) for dz, dx in offsets]
    peers = [z * nx + x for z, x in where]
    for peer in peers:
        pl.semaphore_signal(barrier, inc=1, device_id={"seq": peer}, device_id_type=MESH)

    small = [
        pltpu.make_async_copy(slot_hbm, slot, small_sem.at[0]),
        pltpu.make_async_copy(len_hbm, lens, small_sem.at[1]),
        pltpu.make_async_copy(q_hbm, q_own, small_sem.at[2]),
    ]
    for c in small:
        c.start()
    loads = []
    for s in range(slots):
        kc = pltpu.make_async_copy(k_hbm.at[s], kbuf.at[s], ksem.at[s])
        kc.start()
        loads.append(kc)
    vloads = []
    for s in range(slots):
        vc = pltpu.make_async_copy(v_hbm.at[s], vbuf.at[s], vsem.at[s])
        vc.start()
        vloads.append(vc)
    for c in small:
        c.wait()
    pl.semaphore_wait(barrier, n - 1)

    q_all[me] = q_own[...]
    q_sends = []
    for peer in peers:
        c = pltpu.make_async_remote_copy(
            src_ref=q_own, dst_ref=q_all.at[me], send_sem=q_send_sem, recv_sem=q_recv_sem,
            device_id={"seq": peer}, device_id_type=MESH)
        c.start()

    for s in range(slots):
        loads[s].wait()
        for p in range(pairs):
            ktr[s, p] = kbuf[s, :, p].reshape(wide, hd).T
    for s in range(slots):
        vloads[s].wait()

    rest = q_all.at[pl.ds(0, n - 1)]
    pltpu.make_async_copy(rest, rest, q_recv_sem).wait()

    scale = hd ** -0.5 * math.log2(math.e)
    lane = lax.broadcasted_iota(jnp.int32, (rows, wide), 1)
    row = lax.broadcasted_iota(jnp.int32, (rows, wide), 0)
    matched = lax.rem(lane, half) == row // group
    token = lane // half
    code = [slot[s] for s in range(slots)]
    per_seq = slots * n // nz
    seq = [c // per_seq for c in code]
    left = [lens[b] - lax.rem(c, per_seq) * block for b, c in zip(seq, code)]
    small_lane = lax.broadcasted_iota(jnp.int32, (group, hd), 1)
    small_row = lax.broadcasted_iota(jnp.int32, (group, hd), 0)

    for p in range(pairs):
        peak, total, part = [], [], []
        for s in range(slots):
            q = q_all[pl.ds(seq[s] * nx + p * half, half)].reshape(rows, hd)
            sc = jnp.dot(q, ktr[s, p], preferred_element_type=F32)
            live = matched & (token < left[s])
            sc = jnp.where(live, sc, NEG)
            m = jnp.max(sc, axis=1, keepdims=True)
            w = jnp.where(live, jnp.exp2((sc - m) * scale), 0.0).astype(BF16)
            total.append(jnp.broadcast_to(jnp.sum(w.astype(F32), axis=1, keepdims=True), (rows, hd)))
            part.append(jnp.dot(w, vbuf[s, :, p].reshape(wide, hd), preferred_element_type=F32))
            peak.append(jnp.broadcast_to(m, (rows, hd)))
        for s in range(slots):
            best = peak[s]
            for t in range(slots):
                if t != s:
                    best = jnp.maximum(best, jnp.where(seq[t] == seq[s], peak[t], NEG))
            f = jnp.exp2((peak[s] - best) * scale)
            part[s] = part[s] * f
            total[s] = total[s] * f
        for b in range(nz):
            acc = jnp.zeros((rows, hd), F32)
            den = jnp.zeros((rows, hd), F32)
            top = jnp.full((rows, hd), NEG, F32)
            for s in range(slots):
                mine = seq[s] == b
                acc = acc + jnp.where(mine, part[s], 0.0)
                den = den + jnp.where(mine, total[s], 0.0)
                top = jnp.maximum(top, jnp.where(mine, peak[s], NEG))
            for e in range(half):
                x = p * half + e
                cut = slice(e * group, (e + 1) * group)
                out_send[b, x] = acc[cut].astype(BF16)
                st = jnp.where(small_lane == small_row, top[cut], 0.0)
                st = st + jnp.where(small_lane == small_row + group, den[cut], 0.0)
                st_send[b, x] = jnp.sum(st, axis=0, keepdims=True)
    out_recv[me] = out_send[mz, mx]
    st_recv[me] = st_send[mz, mx]
    for (z, x), peer in zip(where, peers):
        pltpu.make_async_remote_copy(
            src_ref=out_send.at[z, x], dst_ref=out_recv.at[me], send_sem=o_send_sem, recv_sem=o_recv_sem,
            device_id={"seq": peer}, device_id_type=MESH).start()
        pltpu.make_async_remote_copy(
            src_ref=st_send.at[z, x], dst_ref=st_recv.at[me], send_sem=s_send_sem, recv_sem=s_recv_sem,
            device_id={"seq": peer}, device_id_type=MESH).start()

    rest = st_recv.at[pl.ds(0, n - 1)]
    pltpu.make_async_copy(rest, rest, s_recv_sem).wait()
    rest = out_recv.at[pl.ds(0, n - 1)]
    pltpu.make_async_copy(rest, rest, o_recv_sem).wait()

    stat = st_recv[...].reshape(n, hd)
    best = jnp.max(stat, axis=0, keepdims=True)
    f = jnp.exp2((stat - best) * scale)
    den = jnp.sum(f * pltpu.roll(stat, hd - group, 1), axis=0, keepdims=True)
    f = f / den
    acc = jnp.zeros((group, hd), F32)
    for i in range(n):
        g = jnp.where(small_lane == small_row, jnp.broadcast_to(f[i:i + 1], (group, hd)), 0.0)
        g = jnp.sum(g, axis=1, keepdims=True)
        acc = acc + g * out_recv[i].astype(F32)
    o_ref[...] = acc.astype(BF16)

    rest = q_all.at[pl.ds(0, n - 1)]
    pltpu.make_async_copy(rest, rest, q_send_sem).wait()
    rest = out_recv.at[pl.ds(0, n - 1)]
    pltpu.make_async_copy(rest, rest, o_send_sem).wait()
    rest = st_recv.at[pl.ds(0, n - 1)]
    pltpu.make_async_copy(rest, rest, s_send_sem).wait()


def solution(mesh):
    n = mesh.shape["seq"]

    def body(queries, keys, values, lengths, slot_block):
        share, _, hd = queries.shape
        slots, block, kv_local, _ = keys.shape
        nz = lengths.shape[0]
        nx = n // nz
        half = 2
        group = share
        split = (slots, block, nx // half, half, hd)
        any_ = pl.BlockSpec(memory_space=pl.ANY)
        dims = (nz, nx, slots, block, group, hd)
        dma = pltpu.SemaphoreType.DMA
        out = pl.pallas_call(
            functools.partial(attend, dims),
            out_shape=jax.ShapeDtypeStruct((share, hd), BF16),
            in_specs=[any_] * 5,
            out_specs=pl.BlockSpec(memory_space=pltpu.VMEM),
            scratch_shapes=[
                pltpu.VMEM(split, BF16), pltpu.VMEM(split, BF16),
                pltpu.VMEM((slots, nx // half, hd, block * half), BF16),
                pltpu.VMEM((share, hd), BF16), pltpu.VMEM((n, share, hd), BF16), pltpu.VMEM((8, 128), BF16),
                pltpu.SMEM((nz,), jnp.int32), pltpu.SMEM((slots,), jnp.int32),
                pltpu.VMEM((nz, nx, share, hd), BF16), pltpu.VMEM((n, share, hd), BF16),
                pltpu.VMEM((nz, nx, 1, hd), F32), pltpu.VMEM((n, 1, hd), F32),
                dma((slots,)), dma((slots,)), dma((3,)), dma, dma, dma, dma, dma, dma,
            ],
            compiler_params=pltpu.CompilerParams(collective_id=0, has_side_effects=True),
        )(queries.reshape(share, hd), keys.reshape(split), values.reshape(split), lengths, slot_block)
        return out.reshape(share, 1, hd)

    placed = (
        P(("grp", "seq"), "head", None),
        P(("grp", "seq"), None, "head", None),
        P(("grp", "seq"), None, "head", None),
        P("grp"),
        P(("grp", "seq")),
    )
    return jax.shard_map(
        body, mesh=mesh, in_specs=placed, out_specs=P(("grp", "seq"), "head", None), check_vma=False
    )
```

time: 114 us -> 56.1 us (0.49)
  Pallas kernels: 0 us -> 54.8 us
  starting transfers between devices: 35.5 us -> 0 us
  blocking collectives: 34.9 us -> 0 us
  waiting for transfers between devices: 26.7 us -> 0 us
  matrix products: 6.98 us -> 0 us
  local copies, waits for them, and re-layouts: 6.04 us -> 1.26 us
  other arithmetic: 3.3 us -> 0 us
    pallas_call x0 -> x1, Pallas kernels: none -> 54.8 us  [body(): pl.pallas_call(functools.partial(attend, dims), out_shape=jax.ShapeDtypeS...]
    all_to_all x2 -> x0, starting transfers between devices: 35.5 us -> none  [from_everyone(): return lax.all_to_all(copies, axis, split_axis=0, concat_axis=0, tiled=True)]
    all_to_all x1 -> x0, blocking collectives: 34.9 us -> none  [summed_on_arrival(): lax.all_to_all(cut_along(array, dim, length), axis, 0, 0, tiled=True)]
    all_to_all x2 -> x0, waiting for transfers between devices: 26.7 us -> none  [from_everyone(): return lax.all_to_all(copies, axis, split_axis=0, concat_axis=0, tiled=True)]
    dot_general x3 -> x0, matrix products: 6.78 us -> none  [the longest x1 3.51 us: slot_partial(): jnp.einsum('kgd,tkd->kgt', q_one, key_one, preferred_element_type=jnp.flo...]
    gather x3 -> x0, local copies, waits for them, and re-layouts: 1.79 us -> none  [the longest x1 0.64 us: body(): live = positions < jnp.take(lengths, seq_of)[:, None]]
    broadcast_in_dim x1 -> x0, local copies, waits for them, and re-layouts: 1.35 us -> none  [from_everyone(): copies = jnp.broadcast_to(array, (lax.axis_size(axis), *array.shape))]
  transfers between devices with their start and end apart: 2 -> 0, of which waited for: 2 -> 0; matrix products, arithmetic and copies ran while one was open for 4% -> 0% of each run, Pallas kernels for 0% -> 0%
where the time goes in v1:
time: 56.1 us; the launch traced here: 56 us
  Pallas kernels  54.8 us (98%)
  local copies, waits for them, and re-layouts  1.26 us (2%)
    pallas_call x1, Pallas kernels, body(): pl.pallas_call(functools.partial(attend, dims), out_shape=jax.ShapeDtypeS...  54.8 us
    unnamed x1, local copies, waits for them, and re-layouts  1.26 us

profile of v1, /device:TPU:40, one launch (start us, length us, event | category | flops | bytes accessed | tf_op | source)
XLA Modules:
  0.0 56.0 jit_solution(13047401338471473969)
XLA Ops:
  0.0 54.8 %shard_map.55 = bf16[8,128]{1,0:T(8,128)(2,1)} custom-call(bf16[8,128]{1,0:T(8,128)(2,1)} %bitcast.7, bf16[8,512,2,2,128]{4,3,2,1,0:T(2,128)(2,1)} %bitcast.4, bf16[8,512,2,2,128]{4,3,2,1,0:T(2,128)(2,1)} %bitcast.5, s32[16]{0:T(128)} %len_hbm.1, s32[8]{0:T(128)} %slot_hbm.1), custom_call_target="tpu_custom_call" | custom-call | tf_op jit(solution)/shard_map/pallas_call | solution.py:176
  54.8 1.3 %copy.7 = bf16[8,1,128]{2,0,1:T(8,128)(2,1)} copy(bf16[8,1,128]{2,0,1:T(8,128)(2,1)} %bitcast.6) | data formatting | bytes 4096

commit v2 on v1

v2 whole, which is shorter than its diff:
```python
import functools
import math

import jax
import jax.numpy as jnp
from jax import lax
from jax.experimental import pallas as pl
from jax.experimental.pallas import tpu as pltpu
from jax.sharding import PartitionSpec as P

MESH = pl.DeviceIdType.MESH
F32 = jnp.float32
BF16 = jnp.bfloat16
NEG = -1e30


def attend(dims, q_hbm, k_hbm, v_hbm, len_hbm, slot_hbm, o_ref,
           kbuf, vbuf, ktr, q_land, q_use, lens, slot, out_send, out_recv, st_send, st_recv,
           ksem, vsem, small_sem, ready, x_send_sem, x_recv_sem, up_sem, down_sem, block_sem,
           o_send_sem, o_recv_sem, s_send_sem, s_recv_sem):
    nz, nx, slots, block, group, hd = dims
    n = nz * nx
    half = 2
    pairs = nx // half
    rows = half * group
    wide = block * half
    me = lax.axis_index("seq")
    mz, mx = me // nx, lax.rem(me, nx)
    top_z = nz - 1

    def at(z, x):
        return {"seq": z * nx + x}

    barrier = pltpu.get_barrier_semaphore()
    for dx in range(1, nx):
        pl.semaphore_signal(barrier, inc=1, device_id=at(mz, lax.rem(mx + dx, nx)), device_id_type=MESH)

    @pl.when(mz < top_z)
    def _():
        pl.semaphore_signal(barrier, inc=1, device_id=at(mz + 1, mx), device_id_type=MESH)

    small = [
        pltpu.make_async_copy(q_hbm, q_land.at[mz, mx], small_sem.at[2]),
        pltpu.make_async_copy(slot_hbm, slot, small_sem.at[0]),
        pltpu.make_async_copy(len_hbm, lens, small_sem.at[1]),
    ]
    for c in small:
        c.start()
    loads = [pltpu.make_async_copy(k_hbm.at[s], kbuf.at[s], ksem.at[s]) for s in range(slots)]
    vloads = [pltpu.make_async_copy(v_hbm.at[s], vbuf.at[s], vsem.at[s]) for s in range(slots)]
    for c in loads + vloads:
        c.start()
    for c in small:
        c.wait()
    pl.semaphore_wait(barrier, nx - 1 + (mz > 0).astype(jnp.int32))

    @pl.when(mz > 0)
    def _():
        pl.semaphore_signal(ready, inc=1, device_id=at(mz - 1, mx), device_id_type=MESH)

    for dx in range(1, nx):
        pltpu.make_async_remote_copy(
            src_ref=q_land.at[mz, mx], dst_ref=q_land.at[mz, mx], send_sem=x_send_sem, recv_sem=x_recv_sem,
            device_id=at(mz, lax.rem(mx + dx, nx)), device_id_type=MESH).start()
    three = q_land.at[mz, pl.ds(0, nx - 1)]

    def block_copy(b, z, sem):
        return pltpu.make_async_remote_copy(
            src_ref=q_land.at[b], dst_ref=q_land.at[b], send_sem=sem, recv_sem=block_sem.at[b],
            device_id=at(z, mx), device_id_type=MESH)

    def block_wait(b):
        pltpu.make_async_copy(q_land.at[b], q_land.at[b], block_sem.at[b]).wait()

    pltpu.make_async_copy(three, three, x_recv_sem).wait()
    q_use[mz] = q_land[mz]

    @pl.when(mz < top_z)
    def _():
        pl.semaphore_wait(ready, 1)

    for b in range(top_z):
        @pl.when(b < mz)
        def _():
            block_wait(b)

            @pl.when(mz < top_z)
            def _():
                block_copy(b, mz + 1, up_sem.at[b]).start()

            block_copy(mz, b, down_sem.at[b]).start()
            q_use[b] = q_land[b]

    @pl.when(mz < top_z)
    def _():
        block_copy(mz, mz + 1, up_sem.at[mz]).start()

    for s in range(slots):
        loads[s].wait()
        for p in range(pairs):
            ktr[s, p] = kbuf[s, :, p].reshape(wide, hd).T
    for s in range(slots):
        vloads[s].wait()

    scale = hd ** -0.5 * math.log2(math.e)
    per_seq = slots * n // nz
    small_lane = lax.broadcasted_iota(jnp.int32, (group, hd), 1)
    small_row = lax.broadcasted_iota(jnp.int32, (group, hd), 0)

    def one_pass(late, carry):
        @pl.when(late == 1)
        def _():
            for b in range(1, nz):
                @pl.when(b > mz)
                def _():
                    block_wait(b)
                    q_use[b] = q_land[b]

        lane = lax.broadcasted_iota(jnp.int32, (rows, wide), 1)
        row = lax.broadcasted_iota(jnp.int32, (rows, wide), 0)
        matched = lax.rem(lane, half) == row // group
        token = jnp.where(matched, lane // half, block)
        code = [slot[s] for s in range(slots)]
        seq = [c // per_seq for c in code]
        left = []
        for b, c in zip(seq, code):
            rest = jnp.clip(lens[b] - lax.rem(c, per_seq) * block, 0, block)
            ours = (b > mz).astype(jnp.int32) == late
            left.append(jnp.where(ours, rest, 0))
        for p in range(pairs):
            peak, total, part = [], [], []
            for s in range(slots):
                q = q_use[seq[s], pl.ds(p * half, half)].reshape(rows, hd)
                sc = jnp.dot(q, ktr[s, p], preferred_element_type=F32)
                live = token < left[s]
                sc = jnp.where(live, sc, NEG)
                m = jnp.max(sc, axis=1, keepdims=True)
                w = jnp.where(live, jnp.exp2((sc - m) * scale), 0.0).astype(BF16)
                total.append(jnp.broadcast_to(jnp.sum(w.astype(F32), axis=1, keepdims=True), (rows, hd)))
                part.append(jnp.dot(w, vbuf[s, :, p].reshape(wide, hd), preferred_element_type=F32))
                peak.append(jnp.broadcast_to(m, (rows, hd)))
            for s in range(slots):
                best = peak[s]
                for t in range(slots):
                    if t != s:
                        best = jnp.maximum(best, jnp.where(seq[t] == seq[s], peak[t], NEG))
                f = jnp.exp2((peak[s] - best) * scale)
                part[s] = part[s] * f
                total[s] = total[s] * f
            for b in range(nz):
                acc = jnp.zeros((rows, hd), F32)
                den = jnp.zeros((rows, hd), F32)
                top = jnp.full((rows, hd), NEG, F32)
                for s in range(slots):
                    mine = seq[s] == b
                    acc = acc + jnp.where(mine, part[s], 0.0)
                    den = den + jnp.where(mine, total[s], 0.0)
                    top = jnp.maximum(top, jnp.where(mine, peak[s], NEG))
                for e in range(half):
                    x = p * half + e
                    cut = slice(e * group, (e + 1) * group)
                    out_send[late, b, x] = acc[cut].astype(BF16)
                    st = jnp.where(small_lane == small_row, top[cut], 0.0)
                    st = st + jnp.where(small_lane == small_row + group, den[cut], 0.0)
                    st_send[late, b, x] = jnp.sum(st, axis=0, keepdims=True)
            for b in range(nz):
                for e in range(half):
                    x = p * half + e

                    @pl.when(((mz < b).astype(jnp.int32) == late) & (b * nx + x != me))
                    def _():
                        pltpu.make_async_remote_copy(
                            src_ref=out_send.at[late, b, x], dst_ref=out_recv.at[me],
                            send_sem=o_send_sem, recv_sem=o_recv_sem,
                            device_id=at(b, x), device_id_type=MESH).start()
                        pltpu.make_async_remote_copy(
                            src_ref=st_send.at[late, b, x], dst_ref=st_recv.at[me],
                            send_sem=s_send_sem, recv_sem=s_recv_sem,
                            device_id=at(b, x), device_id_type=MESH).start()
        return carry

    lax.fori_loop(0, 2, one_pass, 0)
    out_recv[me] = out_send[0, mz, mx]
    st_recv[me] = st_send[0, mz, mx]

    rest_s = st_recv.at[pl.ds(0, n - 1)]
    rest_o = out_recv.at[pl.ds(0, n - 1)]
    pltpu.make_async_copy(rest_s, rest_s, s_recv_sem).wait()
    pltpu.make_async_copy(rest_o, rest_o, o_recv_sem).wait()

    stat = st_recv[...].reshape(n, hd)
    best = jnp.max(stat, axis=0, keepdims=True)
    f = jnp.exp2((stat - best) * scale)
    den = jnp.sum(f * pltpu.roll(stat, hd - group, 1), axis=0, keepdims=True)
    f = f / den
    acc = jnp.zeros((group, hd), F32)
    for i in range(n):
        g = jnp.where(small_lane == small_row, jnp.broadcast_to(f[i:i + 1], (group, hd)), 0.0)
        g = jnp.sum(g, axis=1, keepdims=True)
        acc = acc + g * out_recv[i].astype(F32)
    o_ref[...] = acc.astype(BF16)

    pltpu.make_async_copy(three, three, x_send_sem).wait()
    for b in range(top_z):
        @pl.when(b < mz)
        def _():
            block_copy(mz, b, down_sem.at[b]).wait_send()

        @pl.when((b <= mz) & (mz < top_z))
        def _():
            block_copy(b, mz + 1, up_sem.at[b]).wait_send()

    pltpu.make_async_copy(rest_o, rest_o, o_send_sem).wait()
    pltpu.make_async_copy(rest_s, rest_s, s_send_sem).wait()


def solution(mesh):
    n = mesh.shape["seq"]

    def body(queries, keys, values, lengths, slot_block):
        share, _, hd = queries.shape
        slots, block, kv_local, _ = keys.shape
        nz = lengths.shape[0]
        nx = n // nz
        half = 2
        group = share
        split = (slots, block, nx // half, half, hd)
        any_ = pl.BlockSpec(memory_space=pl.ANY)
        dims = (nz, nx, slots, block, group, hd)
        dma = pltpu.SemaphoreType.DMA
        out = pl.pallas_call(
            functools.partial(attend, dims),
            out_shape=jax.ShapeDtypeStruct((share, hd), BF16),
            in_specs=[any_] * 5,
            out_specs=pl.BlockSpec(memory_space=pltpu.VMEM),
            scratch_shapes=[
                pltpu.VMEM(split, BF16), pltpu.VMEM(split, BF16),
                pltpu.VMEM((slots, nx // half, hd, block * half), BF16),
                pltpu.VMEM((nz, nx, share, hd), BF16), pltpu.VMEM((nz, nx, share, hd), BF16),
                pltpu.SMEM((nz,), jnp.int32), pltpu.SMEM((slots,), jnp.int32),
                pltpu.VMEM((2, nz, nx, share, hd), BF16), pltpu.VMEM((n, share, hd), BF16),
                pltpu.VMEM((2, nz, nx, 1, hd), F32), pltpu.VMEM((n, 1, hd), F32),
                dma((slots,)), dma((slots,)), dma((3,)), pltpu.SemaphoreType.REGULAR, dma, dma,
                dma((nz,)), dma((nz,)), dma((nz,)), dma, dma, dma, dma,
            ],
            compiler_params=pltpu.CompilerParams(collective_id=0, has_side_effects=True),
        )(queries.reshape(share, hd), keys.reshape(split), values.reshape(split), lengths, slot_block)
        return out.reshape(share, 1, hd)

    placed = (
        P(("grp", "seq"), "head", None),
        P(("grp", "seq"), None, "head", None),
        P(("grp", "seq"), None, "head", None),
        P("grp"),
        P(("grp", "seq")),
    )
    return jax.shard_map(
        body, mesh=mesh, in_specs=placed, out_specs=P(("grp", "seq"), "head", None), check_vma=False
    )
```

time: 56.1 us -> 84.2 us (1.50)
  the two profiles are of different devices: /device:TPU:40 before, /device:TPU:38 now
where the time goes in v2:
time: 84.2 us; the launch traced here: 84.1 us
  Pallas kernels  82.8 us (98%)
  local copies, waits for them, and re-layouts  1.26 us (1%)
    pallas_call x1, Pallas kernels, body(): pl.pallas_call(functools.partial(attend, dims), out_shape=jax.ShapeDtypeS...  82.8 us

profile of v2, /device:TPU:38, one launch (start us, length us, event | category | flops | bytes accessed | tf_op | source)
XLA Modules:
  0.0 84.1 jit_solution(4174346857690977402)
XLA Ops:
  0.0 82.8 %shard_map.55 = bf16[8,128]{1,0:T(8,128)(2,1)} custom-call(bf16[8,128]{1,0:T(8,128)(2,1)} %bitcast.7, bf16[8,512,2,2,128]{4,3,2,1,0:T(2,128)(2,1)} %bitcast.4, bf16[8,512,2,2,128]{4,3,2,1,0:T(2,128)(2,1)} %bitcast.5, s32[16]{0:T(128)} %len_hbm.1, s32[8]{0:T(128)} %slot_hbm.1), custom_call_target="tpu_custom_call" | custom-call | tf_op jit(solution)/shard_map/pallas_call | solution.py:231
  82.8 1.3 %copy.7 = bf16[8,1,128]{2,0,1:T(8,128)(2,1)} copy(bf16[8,1,128]{2,0,1:T(8,128)(2,1)} %bitcast.6) | data formatting | bytes 4096

commit v3 on v2

--- a/solution.py
+++ b/solution.py
@@ -16,7 +16,7 @@
 
 def attend(dims, q_hbm, k_hbm, v_hbm, len_hbm, slot_hbm, o_ref,
            kbuf, vbuf, ktr, q_land, q_use, lens, slot, out_send, out_recv, st_send, st_recv,
-           ksem, vsem, small_sem, ready, x_send_sem, x_recv_sem, up_sem, down_sem, block_sem,
+           ksem, vsem, small_sem, ready, x_ready, x_send_sem, x_recv_sem, block_send, block_sem,
            o_send_sem, o_recv_sem, s_send_sem, s_recv_sem):
     nz, nx, slots, block, group, hd = dims
     n = nz * nx
@@ -32,12 +32,15 @@
         return {"seq": z * nx + x}
 
     barrier = pltpu.get_barrier_semaphore()
-    for dx in range(1, nx):
-        pl.semaphore_signal(barrier, inc=1, device_id=at(mz, lax.rem(mx + dx, nx)), device_id_type=MESH)
-
-    @pl.when(mz < top_z)
-    def _():
-        pl.semaphore_signal(barrier, inc=1, device_id=at(mz + 1, mx), device_id_type=MESH)
+    for z in range(top_z, 0, -1):
+        @pl.when(z > mz)
+        def _():
+            pl.semaphore_signal(barrier, inc=1, device_id=at(z, mx), device_id_type=MESH)
+
+    for x in range(1, nx):
+        @pl.when(x > mx)
+        def _():
+            pl.semaphore_signal(barrier, inc=1, device_id=at(mz, x), device_id_type=MESH)
 
     small = [
         pltpu.make_async_copy(q_hbm, q_land.at[mz, mx], small_sem.at[2]),
@@ -52,16 +55,30 @@
         c.start()
     for c in small:
         c.wait()
-    pl.semaphore_wait(barrier, nx - 1 + (mz > 0).astype(jnp.int32))
-
-    @pl.when(mz > 0)
+    @pl.when(me > 0)
     def _():
-        pl.semaphore_signal(ready, inc=1, device_id=at(mz - 1, mx), device_id_type=MESH)
-
-    for dx in range(1, nx):
-        pltpu.make_async_remote_copy(
-            src_ref=q_land.at[mz, mx], dst_ref=q_land.at[mz, mx], send_sem=x_send_sem, recv_sem=x_recv_sem,
-            device_id=at(mz, lax.rem(mx + dx, nx)), device_id_type=MESH).start()
+        pl.semaphore_wait(barrier, mz + mx)
+
+    for z in range(top_z):
+        @pl.when(z < mz)
+        def _():
+            pl.semaphore_signal(ready.at[mz], inc=1, device_id=at(z, mx), device_id_type=MESH)
+
+    for x in range(nx - 1):
+        @pl.when(x < mx)
+        def _():
+            pl.semaphore_signal(x_ready.at[mx], inc=1, device_id=at(mz, x), device_id_type=MESH)
+
+    for x in range(nx):
+        @pl.when(x > mx)
+        def _():
+            pl.semaphore_wait(x_ready.at[x], 1)
+
+        @pl.when(x != mx)
+        def _():
+            pltpu.make_async_remote_copy(
+                src_ref=q_land.at[mz, mx], dst_ref=q_land.at[mz, mx], send_sem=x_send_sem, recv_sem=x_recv_sem,
+                device_id=at(mz, x), device_id_type=MESH).start()
     three = q_land.at[mz, pl.ds(0, nx - 1)]
 
     def block_copy(b, z, sem):
@@ -75,25 +92,21 @@
     pltpu.make_async_copy(three, three, x_recv_sem).wait()
     q_use[mz] = q_land[mz]
 
-    @pl.when(mz < top_z)
-    def _():
-        pl.semaphore_wait(ready, 1)
-
     for b in range(top_z):
         @pl.when(b < mz)
         def _():
-            block_wait(b)
-
-            @pl.when(mz < top_z)
-            def _():
-                block_copy(b, mz + 1, up_sem.at[b]).start()
-
-            block_copy(mz, b, down_sem.at[b]).start()
-            q_use[b] = q_land[b]
-
-    @pl.when(mz < top_z)
-    def _():
-        block_copy(mz, mz + 1, up_sem.at[mz]).start()
+            block_copy(mz, b, block_send.at[b]).start()
+
+    for z in range(1, nz):
+        @pl.when(z > mz)
+        def _():
+            pl.semaphore_wait(ready.at[z], 1)
+            block_copy(mz, z, block_send.at[z]).start()
+
+    def first(b):
+        d = jnp.abs(mz - b)
+        near = jnp.minimum(d, nz - d) <= nz // 4
+        return ((b <= mz) & ((mz <= nz // 2) | near)).astype(jnp.int32)
 
     for s in range(slots):
         loads[s].wait()
@@ -108,13 +121,11 @@
     small_row = lax.broadcasted_iota(jnp.int32, (group, hd), 0)
 
     def one_pass(late, carry):
-        @pl.when(late == 1)
-        def _():
-            for b in range(1, nz):
-                @pl.when(b > mz)
-                def _():
-                    block_wait(b)
-                    q_use[b] = q_land[b]
+        for b in range(nz):
+            @pl.when((first(b) != late) & (b != mz))
+            def _():
+                block_wait(b)
+                q_use[b] = q_land[b]
 
         lane = lax.broadcasted_iota(jnp.int32, (rows, wide), 1)
         row = lax.broadcasted_iota(jnp.int32, (rows, wide), 0)
@@ -125,7 +136,7 @@
         left = []
         for b, c in zip(seq, code):
             rest = jnp.clip(lens[b] - lax.rem(c, per_seq) * block, 0, block)
-            ours = (b > mz).astype(jnp.int32) == late
+            ours = first(b) != late
             left.append(jnp.where(ours, rest, 0))
         for p in range(pairs):
             peak, total, part = [], [], []
@@ -167,7 +178,7 @@
                 for e in range(half):
                     x = p * half + e
 
-                    @pl.when(((mz < b).astype(jnp.int32) == late) & (b * nx + x != me))
+                    @pl.when((first(b) != late) & (b * nx + x != me))
                     def _():
                         pltpu.make_async_remote_copy(
                             src_ref=out_send.at[late, b, x], dst_ref=out_recv.at[me],
@@ -201,14 +212,10 @@
     o_ref[...] = acc.astype(BF16)
 
     pltpu.make_async_copy(three, three, x_send_sem).wait()
-    for b in range(top_z):
-        @pl.when(b < mz)
-        def _():
-            block_copy(mz, b, down_sem.at[b]).wait_send()
-
-        @pl.when((b <= mz) & (mz < top_z))
-        def _():
-            block_copy(b, mz + 1, up_sem.at[b]).wait_send()
+    for z in range(nz):
+        @pl.when(z != mz)
+        def _():
+            block_copy(mz, z, block_send.at[z]).wait_send()
 
     pltpu.make_async_copy(rest_o, rest_o, o_send_sem).wait()
     pltpu.make_async_copy(rest_s, rest_s, s_send_sem).wait()
@@ -227,7 +234,7 @@
         split = (slots, block, nx // half, half, hd)
         any_ = pl.BlockSpec(memory_space=pl.ANY)
         dims = (nz, nx, slots, block, group, hd)
-        dma = pltpu.SemaphoreType.DMA
+        dma, regular = pltpu.SemaphoreType.DMA, pltpu.SemaphoreType.REGULAR
         out = pl.pallas_call(
             functools.partial(attend, dims),
             out_shape=jax.ShapeDtypeStruct((share, hd), BF16),
@@ -240,8 +247,8 @@
                 pltpu.SMEM((nz,), jnp.int32), pltpu.SMEM((slots,), jnp.int32),
                 pltpu.VMEM((2, nz, nx, share, hd), BF16), pltpu.VMEM((n, share, hd), BF16),
                 pltpu.VMEM((2, nz, nx, 1, hd), F32), pltpu.VMEM((n, 1, hd), F32),
-                dma((slots,)), dma((slots,)), dma((3,)), pltpu.SemaphoreType.REGULAR, dma, dma,
-                dma((nz,)), dma((nz,)), dma((nz,)), dma, dma, dma, dma,
+                dma((slots,)), dma((slots,)), dma((3,)), regular((nz,)), regular((nx,)), dma, dma,
+                dma((nz,)), dma((nz,)), dma, dma, dma, dma,
             ],
             compiler_params=pltpu.CompilerParams(collective_id=0, has_side_effects=True),
         )(queries.reshape(share, hd), keys.reshape(split), values.reshape(split), lengths, slot_block)

time: 84.2 us -> 55.4 us (0.66)
  the two profiles are of different devices: /device:TPU:38 before, /device:TPU:164 now
where the time goes in v3:
time: 55.4 us; the launch traced here: 55.2 us
  Pallas kernels  54 us (97%)
  local copies, waits for them, and re-layouts  1.26 us (2%)
    pallas_call x1, Pallas kernels, body(): pl.pallas_call(functools.partial(attend, dims), out_shape=jax.ShapeDtypeS...  54 us
    unnamed x1, local copies, waits for them, and re-layouts  1.26 us

profile of v3, /device:TPU:164, one launch (start us, length us, event | category | flops | bytes accessed | tf_op | source)
XLA Modules:
  0.0 55.2 jit_solution(13030317739737990115)
XLA Ops:
  0.0 54.0 %shard_map.55 = bf16[8,128]{1,0:T(8,128)(2,1)} custom-call(bf16[8,128]{1,0:T(8,128)(2,1)} %bitcast.7, bf16[8,512,2,2,128]{4,3,2,1,0:T(2,128)(2,1)} %bitcast.4, bf16[8,512,2,2,128]{4,3,2,1,0:T(2,128)(2,1)} %bitcast.5, s32[16]{0:T(128)} %len_hbm.1, s32[8]{0:T(128)} %slot_hbm.1), custom_call_target="tpu_custom_call" | custom-call | tf_op jit(solution)/shard_map/pallas_call | solution.py:238
  54.0 1.3 %copy.7 = bf16[8,1,128]{2,0,1:T(8,128)(2,1)} copy(bf16[8,1,128]{2,0,1:T(8,128)(2,1)} %bitcast.6) | data formatting | bytes 4096

commit v4 on v3

--- a/solution.py
+++ b/solution.py
@@ -15,7 +15,7 @@
 
 
 def attend(dims, q_hbm, k_hbm, v_hbm, len_hbm, slot_hbm, o_ref,
-           kbuf, vbuf, ktr, q_land, q_use, lens, slot, out_send, out_recv, st_send, st_recv,
+           kbuf, vbuf, ktr, gather, gather_stat, q_land, q_use, lens, slot, out_send, out_recv, st_send, st_recv,
            ksem, vsem, small_sem, ready, x_ready, x_send_sem, x_recv_sem, block_send, block_sem,
            o_send_sem, o_recv_sem, s_send_sem, s_recv_sem):
     nz, nx, slots, block, group, hd = dims
@@ -42,33 +42,32 @@
         def _():
             pl.semaphore_signal(barrier, inc=1, device_id=at(mz, x), device_id_type=MESH)
 
+    own = pltpu.make_async_copy(q_hbm, q_land.at[mz, mx], small_sem.at[2])
+    own.start()
+
+    @pl.when(me > 0)
+    def _():
+        pl.semaphore_wait(barrier, mz + mx)
+
+    for z in range(top_z):
+        @pl.when(z < mz)
+        def _():
+            pl.semaphore_signal(ready.at[mz], inc=1, device_id=at(z, mx), device_id_type=MESH)
+
+    for x in range(nx - 1):
+        @pl.when(x < mx)
+        def _():
+            pl.semaphore_signal(x_ready.at[mx], inc=1, device_id=at(mz, x), device_id_type=MESH)
+
     small = [
-        pltpu.make_async_copy(q_hbm, q_land.at[mz, mx], small_sem.at[2]),
         pltpu.make_async_copy(slot_hbm, slot, small_sem.at[0]),
         pltpu.make_async_copy(len_hbm, lens, small_sem.at[1]),
     ]
-    for c in small:
-        c.start()
     loads = [pltpu.make_async_copy(k_hbm.at[s], kbuf.at[s], ksem.at[s]) for s in range(slots)]
     vloads = [pltpu.make_async_copy(v_hbm.at[s], vbuf.at[s], vsem.at[s]) for s in range(slots)]
-    for c in loads + vloads:
+    for c in small + loads + vloads:
         c.start()
-    for c in small:
-        c.wait()
-    @pl.when(me > 0)
-    def _():
-        pl.semaphore_wait(barrier, mz + mx)
-
-    for z in range(top_z):
-        @pl.when(z < mz)
-        def _():
-            pl.semaphore_signal(ready.at[mz], inc=1, device_id=at(z, mx), device_id_type=MESH)
-
-    for x in range(nx - 1):
-        @pl.when(x < mx)
-        def _():
-            pl.semaphore_signal(x_ready.at[mx], inc=1, device_id=at(mz, x), device_id_type=MESH)
-
+    own.wait()
     for x in range(nx):
         @pl.when(x > mx)
         def _():
@@ -104,9 +103,24 @@
             block_copy(mz, z, block_send.at[z]).start()
 
     def first(b):
-        d = jnp.abs(mz - b)
-        near = jnp.minimum(d, nz - d) <= nz // 4
-        return ((b <= mz) & ((mz <= nz // 2) | near)).astype(jnp.int32)
+        return (b <= mz).astype(jnp.int32)
+
+    for c in small:
+        c.wait()
+    per_seq = slots * n // nz
+    code = [slot[s] for s in range(slots)]
+    seq = [c // per_seq for c in code]
+    col = lax.broadcasted_iota(jnp.int32, (1, slots * rows), 1)
+    seq_at = jnp.zeros_like(col)
+    for s in range(slots):
+        seq_at = jnp.where(col // rows == s, seq[s], seq_at)
+    r = lax.broadcasted_iota(jnp.int32, (nz * rows, slots * rows), 0)
+    c = lax.broadcasted_iota(jnp.int32, (nz * rows, slots * rows), 1)
+    gather[...] = jnp.where((r // rows == seq_at) & (lax.rem(r, rows) == lax.rem(c, rows)), 1.0, 0.0).astype(BF16)
+    r = lax.broadcasted_iota(jnp.int32, (nz * half, slots * rows), 0)
+    c = lax.broadcasted_iota(jnp.int32, (nz * half, slots * rows), 1)
+    same = (r // half == seq_at) & (lax.rem(r, half) == lax.rem(c, rows) // group)
+    gather_stat[...] = jnp.where(same, 1.0, 0.0).astype(BF16)
 
     for s in range(slots):
         loads[s].wait()
@@ -116,7 +130,6 @@
         vloads[s].wait()
 
     scale = hd ** -0.5 * math.log2(math.e)
-    per_seq = slots * n // nz
     small_lane = lax.broadcasted_iota(jnp.int32, (group, hd), 1)
     small_row = lax.broadcasted_iota(jnp.int32, (group, hd), 0)
 
@@ -131,8 +144,6 @@
         row = lax.broadcasted_iota(jnp.int32, (rows, wide), 0)
         matched = lax.rem(lane, half) == row // group
         token = jnp.where(matched, lane // half, block)
-        code = [slot[s] for s in range(slots)]
-        seq = [c // per_seq for c in code]
         left = []
         for b, c in zip(seq, code):
             rest = jnp.clip(lens[b] - lax.rem(c, per_seq) * block, 0, block)
@@ -150,6 +161,7 @@
                 total.append(jnp.broadcast_to(jnp.sum(w.astype(F32), axis=1, keepdims=True), (rows, hd)))
                 part.append(jnp.dot(w, vbuf[s, :, p].reshape(wide, hd), preferred_element_type=F32))
                 peak.append(jnp.broadcast_to(m, (rows, hd)))
+            stats = []
             for s in range(slots):
                 best = peak[s]
                 for t in range(slots):
@@ -158,27 +170,27 @@
                 f = jnp.exp2((peak[s] - best) * scale)
                 part[s] = part[s] * f
                 total[s] = total[s] * f
-            for b in range(nz):
-                acc = jnp.zeros((rows, hd), F32)
-                den = jnp.zeros((rows, hd), F32)
-                top = jnp.full((rows, hd), NEG, F32)
-                for s in range(slots):
-                    mine = seq[s] == b
-                    acc = acc + jnp.where(mine, part[s], 0.0)
-                    den = den + jnp.where(mine, total[s], 0.0)
-                    top = jnp.maximum(top, jnp.where(mine, peak[s], NEG))
-                for e in range(half):
-                    x = p * half + e
-                    cut = slice(e * group, (e + 1) * group)
-                    out_send[late, b, x] = acc[cut].astype(BF16)
-                    st = jnp.where(small_lane == small_row, top[cut], 0.0)
-                    st = st + jnp.where(small_lane == small_row + group, den[cut], 0.0)
-                    st_send[late, b, x] = jnp.sum(st, axis=0, keepdims=True)
-            for b in range(nz):
-                for e in range(half):
-                    x = p * half + e
-
-                    @pl.when((first(b) != late) & (b * nx + x != me))
+                head = lax.broadcasted_iota(jnp.int32, (rows, hd), 1) - lax.rem(
+                    lax.broadcasted_iota(jnp.int32, (rows, hd), 0), group)
+                lead = best
+                for t in range(s):
+                    lead = jnp.where(seq[t] == seq[s], 0.0, lead)
+                stats.append(jnp.where(head == 0, lead, 0.0) + jnp.where(head == group, total[s], 0.0))
+            both = jnp.concatenate(part, axis=0).astype(BF16)
+            acc = jnp.dot(gather[...], both, preferred_element_type=F32).astype(BF16)
+            out_send[late, :, pl.ds(p * half, half)] = acc.reshape(nz, half, group, hd)
+            rest = jnp.concatenate(stats, axis=0)
+            st = jnp.zeros((nz * half, hd), F32)
+            for _ in range(3):
+                piece = rest.astype(BF16)
+                st = st + jnp.dot(gather_stat[...], piece, preferred_element_type=F32)
+                rest = rest - piece.astype(F32)
+            st_send[late, :, pl.ds(p * half, half)] = st.reshape(nz, half, 1, hd)
+        for b in range(nz):
+            @pl.when(first(b) != late)
+            def _():
+                for x in range(nx):
+                    @pl.when(b * nx + x != me)
                     def _():
                         pltpu.make_async_remote_copy(
                             src_ref=out_send.at[late, b, x], dst_ref=out_recv.at[me],
@@ -190,7 +202,7 @@
                             device_id=at(b, x), device_id_type=MESH).start()
         return carry
 
-    lax.fori_loop(0, 2, one_pass, 0)
+    lax.fori_loop(0, 1 + (mz < top_z).astype(jnp.int32), one_pass, 0)
     out_recv[me] = out_send[0, mz, mx]
     st_recv[me] = st_send[0, mz, mx]
 
@@ -200,9 +212,11 @@
     pltpu.make_async_copy(rest_o, rest_o, o_recv_sem).wait()
 
     stat = st_recv[...].reshape(n, hd)
+    total = pltpu.roll(stat, hd - group, 1)
+    stat = jnp.where(total > 0.0, stat, NEG)
     best = jnp.max(stat, axis=0, keepdims=True)
     f = jnp.exp2((stat - best) * scale)
-    den = jnp.sum(f * pltpu.roll(stat, hd - group, 1), axis=0, keepdims=True)
+    den = jnp.sum(f * total, axis=0, keepdims=True)
     f = f / den
     acc = jnp.zeros((group, hd), F32)
     for i in range(n):
@@ -243,6 +257,8 @@
             scratch_shapes=[
                 pltpu.VMEM(split, BF16), pltpu.VMEM(split, BF16),
                 pltpu.VMEM((slots, nx // half, hd, block * half), BF16),
+                pltpu.VMEM((nz * half * share, slots * half * share), BF16),
+                pltpu.VMEM((nz * half, slots * half * share), BF16),
                 pltpu.VMEM((nz, nx, share, hd), BF16), pltpu.VMEM((nz, nx, share, hd), BF16),
                 pltpu.SMEM((nz,), jnp.int32), pltpu.SMEM((slots,), jnp.int32),
                 pltpu.VMEM((2, nz, nx, share, hd), BF16), pltpu.VMEM((n, share, hd), BF16),

time: 55.4 us -> 53.2 us (0.960)
  the two profiles are of different devices: /device:TPU:164 before, /device:TPU:38 now
where the time goes in v4:
time: 53.2 us; the launch traced here: 53 us
  Pallas kernels  51.8 us (97%)
  local copies, waits for them, and re-layouts  1.26 us (2%)
    pallas_call x1, Pallas kernels, body(): pl.pallas_call(functools.partial(attend, dims), out_shape=jax.ShapeDtypeS...  51.8 us
    unnamed x1, local copies, waits for them, and re-layouts  1.26 us

profile of v4, /device:TPU:38, one launch (start us, length us, event | category | flops | bytes accessed | tf_op | source)
XLA Modules:
  0.0 53.0 jit_solution(9177097551977036793)
XLA Ops:
  0.0 51.8 %shard_map.55 = bf16[8,128]{1,0:T(8,128)(2,1)} custom-call(bf16[8,128]{1,0:T(8,128)(2,1)} %bitcast.7, bf16[8,512,2,2,128]{4,3,2,1,0:T(2,128)(2,1)} %bitcast.4, bf16[8,512,2,2,128]{4,3,2,1,0:T(2,128)(2,1)} %bitcast.5, s32[16]{0:T(128)} %len_hbm.1, s32[8]{0:T(128)} %slot_hbm.1), custom_call_target="tpu_custom_call" | custom-call | tf_op jit(solution)/shard_map/pallas_call | solution.py:252
  51.8 1.3 %copy.7 = bf16[8,1,128]{2,0,1:T(8,128)(2,1)} copy(bf16[8,1,128]{2,0,1:T(8,128)(2,1)} %bitcast.6) | data formatting | bytes 4096

commit v5 on v4

--- a/solution.py
+++ b/solution.py
@@ -15,9 +15,9 @@
 
 
 def attend(dims, q_hbm, k_hbm, v_hbm, len_hbm, slot_hbm, o_ref,
-           kbuf, vbuf, ktr, gather, gather_stat, q_land, q_use, lens, slot, out_send, out_recv, st_send, st_recv,
+           kbuf, vbuf, ktr, gather, gather_stat, q_land, q_use, lens, slot, out_send, out_recv, st_send, st_recv, z_send, z_recv, zs_send, zs_recv,
            ksem, vsem, small_sem, ready, x_ready, x_send_sem, x_recv_sem, block_send, block_sem,
-           o_send_sem, o_recv_sem, s_send_sem, s_recv_sem):
+           relay_send, o_send_sem, o_recv_sem, s_send_sem, s_recv_sem, z_send_sem, z_recv_sem, zs_send_sem, zs_recv_sem):
     nz, nx, slots, block, group, hd = dims
     n = nz * nx
     half = 2
@@ -28,8 +28,17 @@
     mz, mx = me // nx, lax.rem(me, nx)
     top_z = nz - 1
 
+    reach = nz // 4
+
     def at(z, x):
         return {"seq": z * nx + x}
+
+    def direct(later, earlier):
+        d = later - earlier
+        return (d <= reach) | (d >= nz - reach)
+
+    def relayed(b):
+        return (mz + reach < nz) & (b < mz) & (b > mz - (nz // 2))
 
     barrier = pltpu.get_barrier_semaphore()
     for z in range(top_z, 0, -1):
@@ -50,7 +59,7 @@
         pl.semaphore_wait(barrier, mz + mx)
 
     for z in range(top_z):
-        @pl.when(z < mz)
+        @pl.when((z < mz) & direct(mz, z))
         def _():
             pl.semaphore_signal(ready.at[mz], inc=1, device_id=at(z, mx), device_id_type=MESH)
 
@@ -97,10 +106,17 @@
             block_copy(mz, b, block_send.at[b]).start()
 
     for z in range(1, nz):
-        @pl.when(z > mz)
+        @pl.when((z > mz) & direct(z, mz))
         def _():
             pl.semaphore_wait(ready.at[z], 1)
             block_copy(mz, z, block_send.at[z]).start()
+
+        if z > reach:
+            @pl.when(z == mz + reach)
+            def _():
+                for b in range(max(0, z - reach - nz // 2 + 1), z - reach):
+                    block_wait(b)
+                    block_copy(b, z, relay_send.at[b]).start()
 
     def first(b):
         return (b <= mz).astype(jnp.int32)
@@ -116,10 +132,12 @@
         seq_at = jnp.where(col // rows == s, seq[s], seq_at)
     r = lax.broadcasted_iota(jnp.int32, (nz * rows, slots * rows), 0)
     c = lax.broadcasted_iota(jnp.int32, (nz * rows, slots * rows), 1)
-    gather[...] = jnp.where((r // rows == seq_at) & (lax.rem(r, rows) == lax.rem(c, rows)), 1.0, 0.0).astype(BF16)
+    wanted = r // (nz * group) * group + lax.rem(r, group)
+    same = (lax.rem(r, nz * group) // group == seq_at) & (wanted == lax.rem(c, rows))
+    gather[...] = jnp.where(same, 1.0, 0.0).astype(BF16)
     r = lax.broadcasted_iota(jnp.int32, (nz * half, slots * rows), 0)
     c = lax.broadcasted_iota(jnp.int32, (nz * half, slots * rows), 1)
-    same = (r // half == seq_at) & (lax.rem(r, half) == lax.rem(c, rows) // group)
+    same = (lax.rem(r, nz) == seq_at) & (r // nz == lax.rem(c, rows) // group)
     gather_stat[...] = jnp.where(same, 1.0, 0.0).astype(BF16)
 
     for s in range(slots):
@@ -130,14 +148,21 @@
         vloads[s].wait()
 
     scale = hd ** -0.5 * math.log2(math.e)
-    small_lane = lax.broadcasted_iota(jnp.int32, (group, hd), 1)
-    small_row = lax.broadcasted_iota(jnp.int32, (group, hd), 0)
+
+    def to_rows(f):
+        r = lax.broadcasted_iota(jnp.int32, (nz * group, hd), 0)
+        c = lax.broadcasted_iota(jnp.int32, (nz * group, hd), 1)
+        spread = jnp.broadcast_to(f[:, None, :], (nz, group, hd)).reshape(nz * group, hd)
+        return jnp.sum(jnp.where(lax.rem(r, group) == c, spread, 0.0), axis=1, keepdims=True)
 
     def one_pass(late, carry):
         for b in range(nz):
+            @pl.when((first(b) != late) & (b != mz) & ~relayed(b))
+            def _():
+                block_wait(b)
+
             @pl.when((first(b) != late) & (b != mz))
             def _():
-                block_wait(b)
                 q_use[b] = q_land[b]
 
         lane = lax.broadcasted_iota(jnp.int32, (rows, wide), 1)
@@ -178,61 +203,88 @@
                 stats.append(jnp.where(head == 0, lead, 0.0) + jnp.where(head == group, total[s], 0.0))
             both = jnp.concatenate(part, axis=0).astype(BF16)
             acc = jnp.dot(gather[...], both, preferred_element_type=F32).astype(BF16)
-            out_send[late, :, pl.ds(p * half, half)] = acc.reshape(nz, half, group, hd)
+            for e in range(half):
+                out_send[late, p * half + e] = acc[e * nz * group:(e + 1) * nz * group]
             rest = jnp.concatenate(stats, axis=0)
             st = jnp.zeros((nz * half, hd), F32)
             for _ in range(3):
                 piece = rest.astype(BF16)
                 st = st + jnp.dot(gather_stat[...], piece, preferred_element_type=F32)
                 rest = rest - piece.astype(F32)
-            st_send[late, :, pl.ds(p * half, half)] = st.reshape(nz, half, 1, hd)
+            for e in range(half):
+                st_send[late, p * half + e] = st[e * nz:(e + 1) * nz]
+        for x in range(nx):
+            @pl.when(x != mx)
+            def _():
+                pltpu.make_async_remote_copy(
+                    src_ref=out_send.at[late, x], dst_ref=out_recv.at[late, mx],
+                    send_sem=o_send_sem.at[late], recv_sem=o_recv_sem.at[late],
+                    device_id=at(mz, x), device_id_type=MESH).start()
+                pltpu.make_async_remote_copy(
+                    src_ref=st_send.at[late, x], dst_ref=st_recv.at[late, mx],
+                    send_sem=s_send_sem.at[late], recv_sem=s_recv_sem.at[late],
+                    device_id=at(mz, x), device_id_type=MESH).start()
+        out_recv[late, mx] = out_send[late, mx]
+        st_recv[late, mx] = st_send[late, mx]
+        peers_o = out_recv.at[late, pl.ds(0, nx - 1)]
+        peers_s = st_recv.at[late, pl.ds(0, nx - 1)]
+        pltpu.make_async_copy(peers_s, peers_s, s_recv_sem.at[late]).wait()
+        pltpu.make_async_copy(peers_o, peers_o, o_recv_sem.at[late]).wait()
+
+        stat = [st_recv[late, x] for x in range(nx)]
+        total = [pltpu.roll(v, hd - group, 1) for v in stat]
+        stat = [jnp.where(t > 0.0, v, NEG) for v, t in zip(stat, total)]
+        best = functools.reduce(jnp.maximum, stat)
+        f = [jnp.exp2((v - best) * scale) for v in stat]
+        den = sum(g * t for g, t in zip(f, total))
+        acc = sum(to_rows(f[x]) * out_recv[late, x].astype(F32) for x in range(nx))
+        z_send[late] = acc.reshape(nz, group, hd)
+        lane = lax.broadcasted_iota(jnp.int32, (nz, hd), 1)
+        both = jnp.where(lane < group, best, jnp.where(lane < 2 * group, pltpu.roll(den, group, 1), 0.0))
+        zs_send[late] = both.reshape(nz, 1, hd)
         for b in range(nz):
-            @pl.when(first(b) != late)
-            def _():
-                for x in range(nx):
-                    @pl.when(b * nx + x != me)
-                    def _():
-                        pltpu.make_async_remote_copy(
-                            src_ref=out_send.at[late, b, x], dst_ref=out_recv.at[me],
-                            send_sem=o_send_sem, recv_sem=o_recv_sem,
-                            device_id=at(b, x), device_id_type=MESH).start()
-                        pltpu.make_async_remote_copy(
-                            src_ref=st_send.at[late, b, x], dst_ref=st_recv.at[me],
-                            send_sem=s_send_sem, recv_sem=s_recv_sem,
-                            device_id=at(b, x), device_id_type=MESH).start()
+            @pl.when((first(b) != late) & (b != mz))
+            def _():
+                pltpu.make_async_remote_copy(
+                    src_ref=z_send.at[late, b], dst_ref=z_recv.at[mz], send_sem=z_send_sem, recv_sem=z_recv_sem,
+                    device_id=at(b, mx), device_id_type=MESH).start()
+                pltpu.make_async_remote_copy(
+                    src_ref=zs_send.at[late, b], dst_ref=zs_recv.at[mz], send_sem=zs_send_sem, recv_sem=zs_recv_sem,
+                    device_id=at(b, mx), device_id_type=MESH).start()
+
+        pltpu.make_async_copy(peers_s, peers_s, s_send_sem.at[late]).wait()
+        pltpu.make_async_copy(peers_o, peers_o, o_send_sem.at[late]).wait()
         return carry
 
     lax.fori_loop(0, 1 + (mz < top_z).astype(jnp.int32), one_pass, 0)
-    out_recv[me] = out_send[0, mz, mx]
-    st_recv[me] = st_send[0, mz, mx]
-
-    rest_s = st_recv.at[pl.ds(0, n - 1)]
-    rest_o = out_recv.at[pl.ds(0, n - 1)]
-    pltpu.make_async_copy(rest_s, rest_s, s_recv_sem).wait()
-    pltpu.make_async_copy(rest_o, rest_o, o_recv_sem).wait()
-
-    stat = st_recv[...].reshape(n, hd)
+    z_recv[mz] = z_send[0, mz]
+    zs_recv[mz] = zs_send[0, mz]
+    rest_s = zs_recv.at[pl.ds(0, nz - 1)]
+    rest_z = z_recv.at[pl.ds(0, nz - 1)]
+    pltpu.make_async_copy(rest_s, rest_s, zs_recv_sem).wait()
+    pltpu.make_async_copy(rest_z, rest_z, z_recv_sem).wait()
+
+    stat = zs_recv[...].reshape(nz, hd)
     total = pltpu.roll(stat, hd - group, 1)
     stat = jnp.where(total > 0.0, stat, NEG)
     best = jnp.max(stat, axis=0, keepdims=True)
     f = jnp.exp2((stat - best) * scale)
-    den = jnp.sum(f * total, axis=0, keepdims=True)
-    f = f / den
-    acc = jnp.zeros((group, hd), F32)
-    for i in range(n):
-        g = jnp.where(small_lane == small_row, jnp.broadcast_to(f[i:i + 1], (group, hd)), 0.0)
-        g = jnp.sum(g, axis=1, keepdims=True)
-        acc = acc + g * out_recv[i].astype(F32)
-    o_ref[...] = acc.astype(BF16)
+    f = f / jnp.sum(f * total, axis=0, keepdims=True)
+    acc = to_rows(f) * z_recv[...].reshape(nz * group, hd)
+    o_ref[...] = jnp.sum(acc.reshape(nz, group, hd), axis=0).astype(BF16)
 
     pltpu.make_async_copy(three, three, x_send_sem).wait()
     for z in range(nz):
-        @pl.when(z != mz)
+        @pl.when((z != mz) & ((z < mz) | direct(z, mz)))
         def _():
             block_copy(mz, z, block_send.at[z]).wait_send()
 
-    pltpu.make_async_copy(rest_o, rest_o, o_send_sem).wait()
-    pltpu.make_async_copy(rest_s, rest_s, s_send_sem).wait()
+        @pl.when(relayed(z))
+        def _():
+            block_copy(z, mz + reach, relay_send.at[z]).wait_send()
+
+    pltpu.make_async_copy(rest_z, rest_z, z_send_sem).wait()
+    pltpu.make_async_copy(rest_s, rest_s, zs_send_sem).wait()
 
 
 def solution(mesh):
@@ -261,10 +313,12 @@
                 pltpu.VMEM((nz * half, slots * half * share), BF16),
                 pltpu.VMEM((nz, nx, share, hd), BF16), pltpu.VMEM((nz, nx, share, hd), BF16),
                 pltpu.SMEM((nz,), jnp.int32), pltpu.SMEM((slots,), jnp.int32),
-                pltpu.VMEM((2, nz, nx, share, hd), BF16), pltpu.VMEM((n, share, hd), BF16),
-                pltpu.VMEM((2, nz, nx, 1, hd), F32), pltpu.VMEM((n, 1, hd), F32),
+                pltpu.VMEM((2, nx, nz * share, hd), BF16), pltpu.VMEM((2, nx, nz * share, hd), BF16),
+                pltpu.VMEM((2, nx, nz, hd), F32), pltpu.VMEM((2, nx, nz, hd), F32),
+                pltpu.VMEM((2, nz, share, hd), F32), pltpu.VMEM((nz, share, hd), F32),
+                pltpu.VMEM((2, nz, 1, hd), F32), pltpu.VMEM((nz, 1, hd), F32),
                 dma((slots,)), dma((slots,)), dma((3,)), regular((nz,)), regular((nx,)), dma, dma,
-                dma((nz,)), dma((nz,)), dma, dma, dma, dma,
+                dma((nz,)), dma((nz,)), dma((nz,)), dma((2,)), dma((2,)), dma((2,)), dma((2,)), dma, dma, dma, dma,
             ],
             compiler_params=pltpu.CompilerParams(collective_id=0, has_side_effects=True),
         )(queries.reshape(share, hd), keys.reshape(split), values.reshape(split), lengths, slot_block)

time: 53.2 us -> 60 us (1.13)
  the two profiles are of different devices: /device:TPU:38 before, /device:TPU:34 now
where the time goes in v5:
time: 60 us; the launch traced here: 59.9 us
  Pallas kernels  58.6 us (98%)
  local copies, waits for them, and re-layouts  1.26 us (2%)
    pallas_call x1, Pallas kernels, body(): pl.pallas_call(functools.partial(attend, dims), out_shape=jax.ShapeDtypeS...  58.6 us
    unnamed x1, local copies, waits for them, and re-layouts  1.26 us

profile of v5, /device:TPU:34, one launch (start us, length us, event | category | flops | bytes accessed | tf_op | source)
XLA Modules:
  0.0 59.9 jit_solution(10622303272505948950)
XLA Ops:
  0.0 58.6 %shard_map.55 = bf16[8,128]{1,0:T(8,128)(2,1)} custom-call(bf16[8,128]{1,0:T(8,128)(2,1)} %bitcast.7, bf16[8,512,2,2,128]{4,3,2,1,0:T(2,128)(2,1)} %bitcast.4, bf16[8,512,2,2,128]{4,3,2,1,0:T(2,128)(2,1)} %bitcast.5, s32[16]{0:T(128)} %len_hbm.1, s32[8]{0:T(128)} %slot_hbm.1), custom_call_target="tpu_custom_call" | custom-call | tf_op jit(solution)/shard_map/pallas_call | solution.py:304
  58.6 1.3 %copy.7 = bf16[8,1,128]{2,0,1:T(8,128)(2,1)} copy(bf16[8,1,128]{2,0,1:T(8,128)(2,1)} %bitcast.6) | data formatting | bytes 4096

commit v6 on v5

--- a/solution.py
+++ b/solution.py
@@ -16,7 +16,7 @@
 
 def attend(dims, q_hbm, k_hbm, v_hbm, len_hbm, slot_hbm, o_ref,
            kbuf, vbuf, ktr, gather, gather_stat, q_land, q_use, lens, slot, out_send, out_recv, st_send, st_recv, z_send, z_recv, zs_send, zs_recv,
-           ksem, vsem, small_sem, ready, x_ready, x_send_sem, x_recv_sem, block_send, block_sem,
+           ksem, vsem, small_sem, ready, ready_low, x_ready, root_sem, row_send, row_send_low, root_send, col_send, x_send_sem, x_recv_sem, block_send, block_sem,
            relay_send, o_send_sem, o_recv_sem, s_send_sem, s_recv_sem, z_send_sem, z_recv_sem, zs_send_sem, zs_recv_sem):
     nz, nx, slots, block, group, hd = dims
     n = nz * nx
@@ -40,31 +40,51 @@
     def relayed(b):
         return (mz + reach < nz) & (b < mz) & (b > mz - (nz // 2))
 
+    low = mz == 0
+    root = me == 0
+    agent = me == 1
+
     barrier = pltpu.get_barrier_semaphore()
+
+    def greet(z, x):
+        pl.semaphore_signal(barrier, inc=1, device_id=at(z, x), device_id_type=MESH)
+
     for z in range(top_z, 0, -1):
-        @pl.when(z > mz)
-        def _():
-            pl.semaphore_signal(barrier, inc=1, device_id=at(z, mx), device_id_type=MESH)
-
-    for x in range(1, nx):
-        @pl.when(x > mx)
-        def _():
-            pl.semaphore_signal(barrier, inc=1, device_id=at(mz, x), device_id_type=MESH)
+        @pl.when((z > mz) & ~root)
+        def _():
+            greet(z, mx)
+
+        @pl.when(agent)
+        def _():
+            greet(z, 0)
+
+    for x in range(nx):
+        @pl.when(((x > mx) & ~root) | ((x == 0) & low & ~root))
+        def _():
+            greet(mz, x)
 
     own = pltpu.make_async_copy(q_hbm, q_land.at[mz, mx], small_sem.at[2])
     own.start()
 
-    @pl.when(me > 0)
-    def _():
-        pl.semaphore_wait(barrier, mz + mx)
+    @pl.when(root)
+    def _():
+        pl.semaphore_wait(barrier, nx - 1)
+
+    @pl.when(me > 1)
+    def _():
+        pl.semaphore_wait(barrier, mz + mx - low.astype(jnp.int32))
 
     for z in range(top_z):
-        @pl.when((z < mz) & direct(mz, z))
+        @pl.when((z < mz) & direct(mz, z) & ((mx > 0) | (z > 0)))
         def _():
             pl.semaphore_signal(ready.at[mz], inc=1, device_id=at(z, mx), device_id_type=MESH)
 
+    @pl.when((mx == 0) & ~low & direct(mz, 0))
+    def _():
+        pl.semaphore_signal(ready_low.at[mz], inc=1, device_id=at(0, 1), device_id_type=MESH)
+
     for x in range(nx - 1):
-        @pl.when(x < mx)
+        @pl.when((x < mx) & ((x > 0) | ~low))
         def _():
             pl.semaphore_signal(x_ready.at[mx], inc=1, device_id=at(mz, x), device_id_type=MESH)
 
@@ -77,49 +97,52 @@
     for c in small + loads + vloads:
         c.start()
     own.wait()
+    first_row = q_land.at[0, 0]
+
+    def row_copy(row, z, x, send, recv):
+        return pltpu.make_async_remote_copy(
+            src_ref=row, dst_ref=row, send_sem=send, recv_sem=recv, device_id=at(z, x), device_id_type=MESH)
+
     for x in range(nx):
-        @pl.when(x > mx)
+        @pl.when((x > mx) & ~root)
         def _():
             pl.semaphore_wait(x_ready.at[x], 1)
 
-        @pl.when(x != mx)
-        def _():
-            pltpu.make_async_remote_copy(
-                src_ref=q_land.at[mz, mx], dst_ref=q_land.at[mz, mx], send_sem=x_send_sem, recv_sem=x_recv_sem,
-                device_id=at(mz, x), device_id_type=MESH).start()
+        @pl.when((x != mx) & ((x > 0) | ~low) & ~root)
+        def _():
+            row_copy(q_land.at[mz, mx], mz, x, x_send_sem, x_recv_sem).start()
+
+        @pl.when((x > 0) & root)
+        def _():
+            row_copy(first_row, 0, x, x_send_sem, root_sem).start()
+
     three = q_land.at[mz, pl.ds(0, nx - 1)]
-
-    def block_copy(b, z, sem):
-        return pltpu.make_async_remote_copy(
-            src_ref=q_land.at[b], dst_ref=q_land.at[b], send_sem=sem, recv_sem=block_sem.at[b],
-            device_id=at(z, mx), device_id_type=MESH)
+    two = q_land.at[mz, pl.ds(0, nx - 2)]
+
+    def piece(b):
+        return q_land.at[0, pl.ds(1, nx - 1)] if isinstance(b, int) and b == 0 else q_land.at[b]
+
+    def block_copy(b, z, x, sem):
+        return row_copy(piece(b), z, x, sem, block_sem.at[b])
 
     def block_wait(b):
-        pltpu.make_async_copy(q_land.at[b], q_land.at[b], block_sem.at[b]).wait()
-
-    pltpu.make_async_copy(three, three, x_recv_sem).wait()
-    q_use[mz] = q_land[mz]
+        pltpu.make_async_copy(piece(b), piece(b), block_sem.at[b]).wait()
+
+    q_use[0, 0] = jnp.zeros((group, hd), BF16)
+
+    @pl.when(low & ~root)
+    def _():
+        pltpu.make_async_copy(two, two, x_recv_sem).wait()
+
+    @pl.when(~low)
+    def _():
+        pltpu.make_async_copy(three, three, x_recv_sem).wait()
+        q_use[mz] = q_land[mz]
 
     for b in range(top_z):
-        @pl.when(b < mz)
-        def _():
-            block_copy(mz, b, block_send.at[b]).start()
-
-    for z in range(1, nz):
-        @pl.when((z > mz) & direct(z, mz))
-        def _():
-            pl.semaphore_wait(ready.at[z], 1)
-            block_copy(mz, z, block_send.at[z]).start()
-
-        if z > reach:
-            @pl.when(z == mz + reach)
-            def _():
-                for b in range(max(0, z - reach - nz // 2 + 1), z - reach):
-                    block_wait(b)
-                    block_copy(b, z, relay_send.at[b]).start()
-
-    def first(b):
-        return (b <= mz).astype(jnp.int32)
+        @pl.when((b < mz) & ((mx > 0) | (b > 0)))
+        def _():
+            block_copy(mz, b, mx, block_send.at[b]).start()
 
     for c in small:
         c.wait()
@@ -147,6 +170,55 @@
     for s in range(slots):
         vloads[s].wait()
 
+    for z in range(1, nz):
+        @pl.when((z > mz) & direct(z, mz) & ~root)
+        def _():
+            pl.semaphore_wait(ready.at[z], 1)
+
+            @pl.when(~low)
+            def _():
+                block_copy(mz, z, mx, block_send.at[z]).start()
+
+            @pl.when(low)
+            def _():
+                block_copy(0, z, mx, block_send.at[z]).start()
+
+        if direct(z, 0):
+            @pl.when(agent)
+            def _():
+                pl.semaphore_wait(ready_low.at[z], 1)
+                block_copy(0, z, 0, col_send.at[z]).start()
+
+        if z > reach:
+            @pl.when(z == mz + reach)
+            def _():
+                for b in range(max(0, z - reach - nz // 2 + 1), z - reach):
+                    block_wait(b)
+                    block_copy(b, z, mx, relay_send.at[b]).start()
+
+    @pl.when(low & ~root)
+    def _():
+        pltpu.make_async_copy(first_row, first_row, root_sem).wait()
+
+    for z in range(1, nz):
+        @pl.when(low & ~root)
+        def _():
+            row_copy(first_row, z, mx, row_send.at[z], root_sem).start()
+
+        @pl.when(agent)
+        def _():
+            row_copy(first_row, z, 0, row_send_low.at[z], root_sem).start()
+
+    @pl.when(agent)
+    def _():
+        block_copy(0, 0, 0, root_send.at[0]).start()
+
+    def first(b):
+        return ((b <= mz) & (mz >= reach)).astype(jnp.int32)
+
+    def goes(b, late):
+        return jnp.where((mx == 0) & (b == 0), late == 1, first(b) != late)
+
     scale = hd ** -0.5 * math.log2(math.e)
 
     def to_rows(f):
@@ -157,13 +229,30 @@
 
     def one_pass(late, carry):
         for b in range(nz):
-            @pl.when((first(b) != late) & (b != mz) & ~relayed(b))
+            @pl.when((first(b) != late) & ((b != mz) | root) & ~relayed(b))
             def _():
                 block_wait(b)
 
-            @pl.when((first(b) != late) & (b != mz))
-            def _():
-                q_use[b] = q_land[b]
+            if b > 0:
+                @pl.when(agent)
+                def _():
+                    block_copy(b, 0, 0, root_send.at[b]).start()
+
+                @pl.when((first(b) != late) & (b != mz))
+                def _():
+                    q_use[b] = q_land[b]
+            else:
+                @pl.when(first(b) != late)
+                def _():
+                    q_use[0, pl.ds(1, nx - 1)] = q_land[0, pl.ds(1, nx - 1)]
+
+        @pl.when(late == 1)
+        def _():
+            @pl.when(~low)
+            def _():
+                pltpu.make_async_copy(first_row, first_row, root_sem).wait()
+
+            q_use[0, 0] = q_land[0, 0]
 
         lane = lax.broadcasted_iota(jnp.int32, (rows, wide), 1)
         row = lax.broadcasted_iota(jnp.int32, (rows, wide), 0)
@@ -172,7 +261,7 @@
         left = []
         for b, c in zip(seq, code):
             rest = jnp.clip(lens[b] - lax.rem(c, per_seq) * block, 0, block)
-            ours = first(b) != late
+            ours = (first(b) != late) | ((b == 0) & (late == 1))
             left.append(jnp.where(ours, rest, 0))
         for p in range(pairs):
             peak, total, part = [], [], []
@@ -243,7 +332,7 @@
         both = jnp.where(lane < group, best, jnp.where(lane < 2 * group, pltpu.roll(den, group, 1), 0.0))
         zs_send[late] = both.reshape(nz, 1, hd)
         for b in range(nz):
-            @pl.when((first(b) != late) & (b != mz))
+            @pl.when(goes(b, late) & (b != mz))
             def _():
                 pltpu.make_async_remote_copy(
                     src_ref=z_send.at[late, b], dst_ref=z_recv.at[mz], send_sem=z_send_sem, recv_sem=z_recv_sem,
@@ -256,9 +345,10 @@
         pltpu.make_async_copy(peers_o, peers_o, o_send_sem.at[late]).wait()
         return carry
 
-    lax.fori_loop(0, 1 + (mz < top_z).astype(jnp.int32), one_pass, 0)
-    z_recv[mz] = z_send[0, mz]
-    zs_recv[mz] = zs_send[0, mz]
+    lax.fori_loop((mz < reach).astype(jnp.int32), 2, one_pass, 0)
+    last = (mz < reach).astype(jnp.int32)
+    z_recv[mz] = z_send[last, mz]
+    zs_recv[mz] = zs_send[last, mz]
     rest_s = zs_recv.at[pl.ds(0, nz - 1)]
     rest_z = z_recv.at[pl.ds(0, nz - 1)]
     pltpu.make_async_copy(rest_s, rest_s, zs_recv_sem).wait()
@@ -273,15 +363,44 @@
     acc = to_rows(f) * z_recv[...].reshape(nz * group, hd)
     o_ref[...] = jnp.sum(acc.reshape(nz, group, hd), axis=0).astype(BF16)
 
-    pltpu.make_async_copy(three, three, x_send_sem).wait()
+    @pl.when(low & ~root)
+    def _():
+        pltpu.make_async_copy(two, two, x_send_sem).wait()
+
+    @pl.when(root | ~low)
+    def _():
+        pltpu.make_async_copy(three, three, x_send_sem).wait()
+
     for z in range(nz):
-        @pl.when((z != mz) & ((z < mz) | direct(z, mz)))
-        def _():
-            block_copy(mz, z, block_send.at[z]).wait_send()
+        @pl.when(~low & (z != mz) & (((z < mz) & ((mx > 0) | (z > 0))) | ((z > mz) & direct(z, mz))))
+        def _():
+            block_copy(mz, z, mx, block_send.at[z]).wait_send()
 
         @pl.when(relayed(z))
         def _():
-            block_copy(z, mz + reach, relay_send.at[z]).wait_send()
+            block_copy(z, 0, mx, relay_send.at[z]).wait_send()
+
+        @pl.when(agent)
+        def _():
+            block_copy(z, 0, 0, root_send.at[z]).wait_send()
+
+        if z > 0:
+            @pl.when(low & ~root)
+            def _():
+                row_copy(first_row, z, mx, row_send.at[z], root_sem).wait_send()
+
+            @pl.when(agent)
+            def _():
+                row_copy(first_row, z, 0, row_send_low.at[z], root_sem).wait_send()
+
+            if direct(z, 0):
+                @pl.when(low & ~root)
+                def _():
+                    block_copy(0, z, mx, block_send.at[z]).wait_send()
+
+                @pl.when(agent)
+                def _():
+                    block_copy(0, z, 0, col_send.at[z]).wait_send()
 
     pltpu.make_async_copy(rest_z, rest_z, z_send_sem).wait()
     pltpu.make_async_copy(rest_s, rest_s, zs_send_sem).wait()
@@ -317,7 +436,7 @@
                 pltpu.VMEM((2, nx, nz, hd), F32), pltpu.VMEM((2, nx, nz, hd), F32),
                 pltpu.VMEM((2, nz, share, hd), F32), pltpu.VMEM((nz, share, hd), F32),
                 pltpu.VMEM((2, nz, 1, hd), F32), pltpu.VMEM((nz, 1, hd), F32),
-                dma((slots,)), dma((slots,)), dma((3,)), regular((nz,)), regular((nx,)), dma, dma,
+                dma((slots,)), dma((slots,)), dma((3,)), regular((nz,)), regular((nz,)), regular((nx,)), dma, dma((nz,)), dma((nz,)), dma((nz,)), dma((nz,)), dma, dma,
                 dma((nz,)), dma((nz,)), dma((nz,)), dma((2,)), dma((2,)), dma((2,)), dma((2,)), dma, dma, dma, dma,
             ],
             compiler_params=pltpu.CompilerParams(collective_id=0, has_side_effects=True),

time: 60 us -> 64.7 us (1.078)
  the two profiles are of different devices: /device:TPU:34 before, /device:TPU:40 now
where the time goes in v6:
time: 64.7 us; the launch traced here: 64.6 us
  Pallas kernels  63.3 us (98%)
  local copies, waits for them, and re-layouts  1.26 us (2%)
    pallas_call x1, Pallas kernels, body(): pl.pallas_call(functools.partial(attend, dims), out_shape=jax.ShapeDtypeS...  63.3 us

profile of v6, /device:TPU:40, one launch (start us, length us, event | category | flops | bytes accessed | tf_op | source)
XLA Modules:
  0.0 64.6 jit_solution(5791950811650723221)
XLA Ops:
  0.0 63.3 %shard_map.55 = bf16[8,128]{1,0:T(8,128)(2,1)} custom-call(bf16[8,128]{1,0:T(8,128)(2,1)} %bitcast.7, bf16[8,512,2,2,128]{4,3,2,1,0:T(2,128)(2,1)} %bitcast.4, bf16[8,512,2,2,128]{4,3,2,1,0:T(2,128)(2,1)} %bitcast.5, s32[16]{0:T(128)} %len_hbm.1, s32[8]{0:T(128)} %slot_hbm.1), custom_call_target="tpu_custom_call" | custom-call | tf_op jit(solution)/shard_map/pallas_call | solution.py:423
  63.3 1.3 %copy.7 = bf16[8,1,128]{2,0,1:T(8,128)(2,1)} copy(bf16[8,1,128]{2,0,1:T(8,128)(2,1)} %bitcast.6) | data formatting | bytes 4096

commit v7 on v6

v7 whole, which is shorter than its diff:
```python
import functools
import math

import jax
import jax.numpy as jnp
from jax import lax
from jax.experimental import pallas as pl
from jax.experimental.pallas import tpu as pltpu
from jax.sharding import PartitionSpec as P

MESH = pl.DeviceIdType.MESH
F32 = jnp.float32
BF16 = jnp.bfloat16
NEG = -1e30


def attend(dims, q_hbm, k_hbm, v_hbm, len_hbm, slot_hbm, o_ref,
           kbuf, vbuf, ktr, gather, gather_stat, q_land, q_use, lens, slot, out_send, out_recv, st_send, st_recv,
           ksem, vsem, small_sem, ready, ready_low, x_ready, root_sem, row_send, row_send_low, root_send, col_send, x_send_sem, x_recv_sem, block_send, block_sem,
           o_send_sem, o_recv_sem, s_send_sem, s_recv_sem):
    nz, nx, slots, block, group, hd = dims
    n = nz * nx
    half = 2
    pairs = nx // half
    rows = half * group
    wide = block * half
    me = lax.axis_index("seq")
    mz, mx = me // nx, lax.rem(me, nx)
    top_z = nz - 1

    reach = nz // 4
    middle = nz // 2

    def at(z, x):
        return {"seq": z * nx + x}

    low = mz == 0
    root = me == 0
    agent = me == 1

    barrier = pltpu.get_barrier_semaphore()

    def greet(z, x):
        pl.semaphore_signal(barrier, inc=1, device_id=at(z, x), device_id_type=MESH)

    for z in range(top_z, 0, -1):
        @pl.when((z > mz) & ~root)
        def _():
            greet(z, mx)

        @pl.when(agent)
        def _():
            greet(z, 0)

    for x in range(nx):
        @pl.when(((x > mx) & ~root) | ((x == 0) & low & ~root))
        def _():
            greet(mz, x)

    own = pltpu.make_async_copy(q_hbm, q_land.at[mz, mx], small_sem.at[2])
    own.start()

    @pl.when(root)
    def _():
        pl.semaphore_wait(barrier, nx - 1)

    @pl.when(me > 1)
    def _():
        pl.semaphore_wait(barrier, mz + mx - low.astype(jnp.int32))

    for z in range(top_z):
        @pl.when((z < mz) & ((mx > 0) | (z > 0)))
        def _():
            pl.semaphore_signal(ready.at[mz], inc=1, device_id=at(z, mx), device_id_type=MESH)

    @pl.when((mx == 0) & ~low)
    def _():
        pl.semaphore_signal(ready_low.at[mz], inc=1, device_id=at(0, 1), device_id_type=MESH)

    for x in range(nx - 1):
        @pl.when((x < mx) & ((x > 0) | ~low))
        def _():
            pl.semaphore_signal(x_ready.at[mx], inc=1, device_id=at(mz, x), device_id_type=MESH)

    small = [
        pltpu.make_async_copy(slot_hbm, slot, small_sem.at[0]),
        pltpu.make_async_copy(len_hbm, lens, small_sem.at[1]),
    ]
    loads = [pltpu.make_async_copy(k_hbm.at[s], kbuf.at[s], ksem.at[s]) for s in range(slots)]
    vloads = [pltpu.make_async_copy(v_hbm.at[s], vbuf.at[s], vsem.at[s]) for s in range(slots)]
    for c in small + loads + vloads:
        c.start()
    own.wait()
    first_row = q_land.at[0, 0]

    def row_copy(row, z, x, send, recv):
        return pltpu.make_async_remote_copy(
            src_ref=row, dst_ref=row, send_sem=send, recv_sem=recv, device_id=at(z, x), device_id_type=MESH)

    for x in range(nx):
        @pl.when((x > mx) & ~root)
        def _():
            pl.semaphore_wait(x_ready.at[x], 1)

        @pl.when((x != mx) & ((x > 0) | ~low) & ~root)
        def _():
            row_copy(q_land.at[mz, mx], mz, x, x_send_sem, x_recv_sem).start()

        @pl.when((x > 0) & root)
        def _():
            row_copy(first_row, 0, x, x_send_sem, root_sem).start()

    three = q_land.at[mz, pl.ds(0, nx - 1)]
    two = q_land.at[mz, pl.ds(0, nx - 2)]

    def piece(b):
        return q_land.at[0, pl.ds(1, nx - 1)] if isinstance(b, int) and b == 0 else q_land.at[b]

    def block_copy(b, z, x, sem):
        return row_copy(piece(b), z, x, sem, block_sem.at[b])

    def block_wait(b):
        pltpu.make_async_copy(piece(b), piece(b), block_sem.at[b]).wait()

    q_use[0, 0] = jnp.zeros((group, hd), BF16)

    @pl.when(low & ~root)
    def _():
        pltpu.make_async_copy(two, two, x_recv_sem).wait()

    @pl.when(~low)
    def _():
        pltpu.make_async_copy(three, three, x_recv_sem).wait()
        q_use[mz] = q_land[mz]

    for b in range(top_z):
        @pl.when((b < mz) & ((mx > 0) | (b > 0)))
        def _():
            block_copy(mz, b, mx, block_send.at[b]).start()

    for z in range(1, nz):
        @pl.when((z > mz) & ~root)
        def _():
            pl.semaphore_wait(ready.at[z], 1)

            @pl.when(~low)
            def _():
                block_copy(mz, z, mx, block_send.at[z]).start()

            @pl.when(low)
            def _():
                block_copy(0, z, mx, block_send.at[z]).start()

        @pl.when(agent)
        def _():
            pl.semaphore_wait(ready_low.at[z], 1)
            block_copy(0, z, 0, col_send.at[z]).start()

    @pl.when(low & ~root)
    def _():
        pltpu.make_async_copy(first_row, first_row, root_sem).wait()

    for z in range(1, nz):
        @pl.when(low & ~root)
        def _():
            row_copy(first_row, z, mx, row_send.at[z], root_sem).start()

        @pl.when(agent)
        def _():
            row_copy(first_row, z, 0, row_send_low.at[z], root_sem).start()

    @pl.when(agent)
    def _():
        block_copy(0, 0, 0, root_send.at[0]).start()

    for c in small:
        c.wait()
    per_seq = slots * n // nz
    code = [slot[s] for s in range(slots)]
    seq = [c // per_seq for c in code]
    col = lax.broadcasted_iota(jnp.int32, (1, slots * rows), 1)
    seq_at = jnp.zeros_like(col)
    for s in range(slots):
        seq_at = jnp.where(col // rows == s, seq[s], seq_at)
    r = lax.broadcasted_iota(jnp.int32, (nz * rows, slots * rows), 0)
    c = lax.broadcasted_iota(jnp.int32, (nz * rows, slots * rows), 1)
    wanted = r // (nz * group) * group + lax.rem(r, group)
    same = (lax.rem(r, nz * group) // group == seq_at) & (wanted == lax.rem(c, rows))
    gather[...] = jnp.where(same, 1.0, 0.0).astype(BF16)
    lane_slot = lax.broadcasted_iota(jnp.int32, (1, hd), 1)
    lane_seq = jnp.full((1, hd), -1, jnp.int32)
    lane_lead = jnp.zeros((1, hd), jnp.int32)
    for s in range(slots):
        lead = 1
        for t in range(s):
            lead = lead * (seq[t] != seq[s]).astype(jnp.int32)
        lane_seq = jnp.where(lax.rem(lane_slot, slots) == s, seq[s], lane_seq)
        lane_lead = jnp.where(lane_slot == s, lead, lane_lead)
    lane_seq = jnp.where(lane_slot < 3 * slots, lane_seq, -1)
    r = lax.broadcasted_iota(jnp.int32, (nz, hd), 0)
    gather_stat[...] = jnp.where(r == lane_seq, 1.0, 0.0).astype(BF16)

    for s in range(slots):
        loads[s].wait()
        for p in range(pairs):
            ktr[s, p] = kbuf[s, :, p].reshape(wide, hd).T
    for s in range(slots):
        vloads[s].wait()

    row_pass = (mz < middle).astype(jnp.int32)

    def first(b):
        d = jnp.abs(mz - b)
        near = jnp.minimum(d, nz - d) <= jnp.maximum(nz - mz, reach + 1)
        return ((b <= mz) & (mz >= reach) & near).astype(jnp.int32)

    def goes(b, x, late):
        return late == row_pass if b == 0 and x == 0 else first(b) != late

    scale = hd ** -0.5 * math.log2(math.e)

    def one_pass(late, carry):
        for b in range(nz):
            @pl.when((first(b) != late) & ((b != mz) | root))
            def _():
                block_wait(b)

            if b > 0:
                @pl.when(agent)
                def _():
                    block_copy(b, 0, 0, root_send.at[b]).start()

                @pl.when((first(b) != late) & (b != mz))
                def _():
                    q_use[b] = q_land[b]
            else:
                @pl.when(first(b) != late)
                def _():
                    q_use[0, pl.ds(1, nx - 1)] = q_land[0, pl.ds(1, nx - 1)]

        @pl.when(late == row_pass)
        def _():
            @pl.when(~low)
            def _():
                pltpu.make_async_copy(first_row, first_row, root_sem).wait()

            q_use[0, 0] = q_land[0, 0]

        lane = lax.broadcasted_iota(jnp.int32, (rows, wide), 1)
        row = lax.broadcasted_iota(jnp.int32, (rows, wide), 0)
        matched = lax.rem(lane, half) == row // group
        token = jnp.where(matched, lane // half, block)
        left = []
        for b, c in zip(seq, code):
            rest = jnp.clip(lens[b] - lax.rem(c, per_seq) * block, 0, block)
            ours = (first(b) != late) | ((b == 0) & (late == row_pass))
            left.append(jnp.where(ours, rest, 0))
        for p in range(pairs):
            peak, total, part = [], [], []
            for s in range(slots):
                q = q_use[seq[s], pl.ds(p * half, half)].reshape(rows, hd)
                sc = jnp.dot(q, ktr[s, p], preferred_element_type=F32)
                live = token < left[s]
                sc = jnp.where(live, sc, NEG)
                m = jnp.max(sc, axis=1, keepdims=True)
                w = jnp.where(live, jnp.exp2((sc - m) * scale), 0.0).astype(BF16)
                total.append(jnp.sum(w.astype(F32), axis=1, keepdims=True))
                part.append(jnp.dot(w, vbuf[s, :, p].reshape(wide, hd), preferred_element_type=F32))
                peak.append(m)
            lane_s = lax.broadcasted_iota(jnp.int32, (rows, hd), 1)
            tops = jnp.full((rows, hd), NEG, F32)
            sums = jnp.zeros((rows, hd), F32)
            best = jnp.full((rows, hd), NEG, F32)
            for s in range(slots):
                tops = jnp.where(lane_s == s, peak[s], tops)
                sums = jnp.where(lane_s == s, total[s], sums)
                best = jnp.maximum(best, jnp.where(lane_seq == seq[s], peak[s], NEG))
            f = jnp.exp2((tops - best) * scale)
            sums = sums * f
            lead = jnp.where(lane_lead == 1, best, 0.0)
            both = jnp.concatenate([part[s] * f[:, s:s + 1] for s in range(slots)], axis=0).astype(BF16)
            acc = jnp.dot(gather[...], both, preferred_element_type=F32)
            for e in range(half):
                half_acc = acc[e * nz * group:(e + 1) * nz * group].reshape(nz, group, hd)
                out_send[late, p * half + e] = half_acc.astype(BF16)
            mixed = []
            for e in range(half):
                mixed += [lead[e * group:(e + 1) * group], sums[e * group:(e + 1) * group]]
            rest = jnp.concatenate(mixed + [jnp.zeros((hd - 2 * rows, hd), F32)], axis=0)
            packed = jnp.zeros((hd, hd), F32)
            for k in range(3):
                coarse = rest.astype(BF16).astype(F32)
                packed = packed + (pltpu.roll(coarse, k * slots, 1) if k else coarse)
                rest = rest - coarse
            st = lax.dot_general(
                gather_stat[...], packed.astype(BF16), (((1,), (1,)), ((), ())), preferred_element_type=F32)
            st_send[late, p] = st.reshape(nz, 1, hd)
        for b in range(nz):
            for x in range(nx):
                @pl.when(goes(b, x, late) & (b * nx + x != me))
                def _():
                    pltpu.make_async_remote_copy(
                        src_ref=out_send.at[late, x, b], dst_ref=out_recv.at[me],
                        send_sem=o_send_sem, recv_sem=o_recv_sem,
                        device_id=at(b, x), device_id_type=MESH).start()
                    pltpu.make_async_remote_copy(
                        src_ref=st_send.at[late, x // half, b], dst_ref=st_recv.at[me],
                        send_sem=s_send_sem, recv_sem=s_recv_sem,
                        device_id=at(b, x), device_id_type=MESH).start()
        return carry

    lax.fori_loop((mz < reach).astype(jnp.int32), 2, one_pass, 0)
    last = (mz < reach).astype(jnp.int32)
    out_recv[me] = out_send[last, mx, mz]
    st_recv[me] = st_send[last, mx // half, mz]
    rest_s = st_recv.at[pl.ds(0, n - 1)]
    rest_o = out_recv.at[pl.ds(0, n - 1)]
    pltpu.make_async_copy(rest_s, rest_s, s_recv_sem).wait()
    pltpu.make_async_copy(rest_o, rest_o, o_recv_sem).wait()

    stat = st_recv[...].reshape(n, hd)
    stat = jnp.where(lax.rem(mx, half) == 1, pltpu.roll(stat, hd - 2 * group, 1), stat)
    total = pltpu.roll(stat, hd - group, 1)
    stat = jnp.where(total > 0.0, stat, NEG)
    best = jnp.max(stat, axis=0, keepdims=True)
    f = jnp.exp2((stat - best) * scale)
    f = f / jnp.sum(f * total, axis=0, keepdims=True)
    r = lax.broadcasted_iota(jnp.int32, (group, hd), 0)
    c = lax.broadcasted_iota(jnp.int32, (group, hd), 1)
    acc = jnp.zeros((group, hd), F32)
    for i in range(n):
        g = jnp.where(c == r, jnp.broadcast_to(f[i:i + 1], (group, hd)), 0.0)
        acc = acc + jnp.sum(g, axis=1, keepdims=True) * out_recv[i].astype(F32)
    o_ref[...] = acc.astype(BF16)

    @pl.when(low & ~root)
    def _():
        pltpu.make_async_copy(two, two, x_send_sem).wait()

    @pl.when(root | ~low)
    def _():
        pltpu.make_async_copy(three, three, x_send_sem).wait()

    for z in range(nz):
        @pl.when(~low & (z != mz) & (((z < mz) & ((mx > 0) | (z > 0))) | (z > mz)))
        def _():
            block_copy(mz, z, mx, block_send.at[z]).wait_send()

        @pl.when(agent)
        def _():
            block_copy(z, 0, 0, root_send.at[z]).wait_send()

        if z > 0:
            @pl.when(low & ~root)
            def _():
                row_copy(first_row, z, mx, row_send.at[z], root_sem).wait_send()

            @pl.when(agent)
            def _():
                row_copy(first_row, z, 0, row_send_low.at[z], root_sem).wait_send()

            @pl.when(low & ~root)
            def _():
                block_copy(0, z, mx, block_send.at[z]).wait_send()

            @pl.when(agent)
            def _():
                block_copy(0, z, 0, col_send.at[z]).wait_send()

    pltpu.make_async_copy(rest_o, rest_o, o_send_sem).wait()
    pltpu.make_async_copy(rest_s, rest_s, s_send_sem).wait()


def solution(mesh):
    n = mesh.shape["seq"]

    def body(queries, keys, values, lengths, slot_block):
        share, _, hd = queries.shape
        slots, block, kv_local, _ = keys.shape
        nz = lengths.shape[0]
        nx = n // nz
        half = 2
        group = share
        split = (slots, block, nx // half, half, hd)
        any_ = pl.BlockSpec(memory_space=pl.ANY)
        dims = (nz, nx, slots, block, group, hd)
        dma, regular = pltpu.SemaphoreType.DMA, pltpu.SemaphoreType.REGULAR
        out = pl.pallas_call(
            functools.partial(attend, dims),
            out_shape=jax.ShapeDtypeStruct((share, hd), BF16),
            in_specs=[any_] * 5,
            out_specs=pl.BlockSpec(memory_space=pltpu.VMEM),
            scratch_shapes=[
                pltpu.VMEM(split, BF16), pltpu.VMEM(split, BF16),
                pltpu.VMEM((slots, nx // half, hd, block * half), BF16),
                pltpu.VMEM((nz * half * share, slots * half * share), BF16),
                pltpu.VMEM((nz, hd), BF16),
                pltpu.VMEM((nz, nx, share, hd), BF16), pltpu.VMEM((nz, nx, share, hd), BF16),
                pltpu.SMEM((nz,), jnp.int32), pltpu.SMEM((slots,), jnp.int32),
                pltpu.VMEM((2, nx, nz, share, hd), BF16), pltpu.VMEM((n, share, hd), BF16),
                pltpu.VMEM((2, nx // half, nz, 1, hd), F32), pltpu.VMEM((n, 1, hd), F32),
                dma((slots,)), dma((slots,)), dma((3,)), regular((nz,)), regular((nz,)), regular((nx,)), dma, dma((nz,)), dma((nz,)), dma((nz,)), dma((nz,)), dma, dma,
                dma((nz,)), dma((nz,)), dma, dma, dma, dma,
            ],
            compiler_params=pltpu.CompilerParams(collective_id=0, has_side_effects=True),
        )(queries.reshape(share, hd), keys.reshape(split), values.reshape(split), lengths, slot_block)
        return out.reshape(share, 1, hd)

    placed = (
        P(("grp", "seq"), "head", None),
        P(("grp", "seq"), None, "head", None),
        P(("grp", "seq"), None, "head", None),
        P("grp"),
        P(("grp", "seq")),
    )
    return jax.shard_map(
        body, mesh=mesh, in_specs=placed, out_specs=P(("grp", "seq"), "head", None), check_vma=False
    )
```

time: 64.7 us -> 55.4 us (0.86)
  the two profiles are of different devices: /device:TPU:40 before, /device:TPU:168 now
where the time goes in v7:
time: 55.4 us; the launch traced here: 55.3 us
  Pallas kernels  54 us (97%)
  local copies, waits for them, and re-layouts  1.26 us (2%)
    pallas_call x1, Pallas kernels, body(): pl.pallas_call(functools.partial(attend, dims), out_shape=jax.ShapeDtypeS...  54 us
    unnamed x1, local copies, waits for them, and re-layouts  1.26 us

profile of v7, /device:TPU:168, one launch (start us, length us, event | category | flops | bytes accessed | tf_op | source)
XLA Modules:
  0.0 55.3 jit_solution(12667082084127042462)
XLA Ops:
  0.0 54.0 %shard_map.55 = bf16[8,128]{1,0:T(8,128)(2,1)} custom-call(bf16[8,128]{1,0:T(8,128)(2,1)} %bitcast.7, bf16[8,512,2,2,128]{4,3,2,1,0:T(2,128)(2,1)} %bitcast.4, bf16[8,512,2,2,128]{4,3,2,1,0:T(2,128)(2,1)} %bitcast.5, s32[16]{0:T(128)} %len_hbm.1, s32[8]{0:T(128)} %slot_hbm.1), custom_call_target="tpu_custom_call" | custom-call | tf_op jit(solution)/shard_map/pallas_call | solution.py:388
  54.0 1.3 %copy.7 = bf16[8,1,128]{2,0,1:T(8,128)(2,1)} copy(bf16[8,1,128]{2,0,1:T(8,128)(2,1)} %bitcast.6) | data formatting | bytes 4096

commit v8 on v7

--- a/solution.py
+++ b/solution.py
@@ -207,11 +207,11 @@
     for s in range(slots):
         vloads[s].wait()
 
-    row_pass = (mz < middle).astype(jnp.int32)
+    row_pass = (mz < reach).astype(jnp.int32)
 
     def first(b):
         d = jnp.abs(mz - b)
-        near = jnp.minimum(d, nz - d) <= jnp.maximum(nz - mz, reach + 1)
+        near = (mz <= middle) | (b < reach) | (jnp.minimum(d, nz - d) <= reach + 1)
         return ((b <= mz) & (mz >= reach) & near).astype(jnp.int32)
 
     def goes(b, x, late):
@@ -255,18 +255,32 @@
             rest = jnp.clip(lens[b] - lax.rem(c, per_seq) * block, 0, block)
             ours = (first(b) != late) | ((b == 0) & (late == row_pass))
             left.append(jnp.where(ours, rest, 0))
+        work = [(p, s) for p in range(pairs) for s in range(slots)]
+
+        def score(p, s):
+            q = q_use[seq[s], pl.ds(p * half, half)].reshape(rows, hd)
+            return jnp.dot(q, ktr[s, p], preferred_element_type=F32)
+
+        def soften(sc, s):
+            live = token < left[s]
+            sc = jnp.where(live, sc, NEG)
+            m = jnp.max(sc, axis=1, keepdims=True)
+            w = jnp.where(live, jnp.exp2((sc - m) * scale), 0.0).astype(BF16)
+            return m, jnp.sum(w.astype(F32), axis=1, keepdims=True), w
+
+        peaks, totals, weights, parts = {}, {}, {}, {}
+        scores = {}
+        for i in range(len(work) + 2):
+            if i < len(work):
+                scores[i] = score(*work[i])
+            if 0 <= i - 1 < len(work):
+                peaks[i - 1], totals[i - 1], weights[i - 1] = soften(scores.pop(i - 1), work[i - 1][1])
+            if i >= 2:
+                p, s = work[i - 2]
+                parts[i - 2] = jnp.dot(
+                    weights.pop(i - 2), vbuf[s, :, p].reshape(wide, hd), preferred_element_type=F32)
         for p in range(pairs):
-            peak, total, part = [], [], []
-            for s in range(slots):
-                q = q_use[seq[s], pl.ds(p * half, half)].reshape(rows, hd)
-                sc = jnp.dot(q, ktr[s, p], preferred_element_type=F32)
-                live = token < left[s]
-                sc = jnp.where(live, sc, NEG)
-                m = jnp.max(sc, axis=1, keepdims=True)
-                w = jnp.where(live, jnp.exp2((sc - m) * scale), 0.0).astype(BF16)
-                total.append(jnp.sum(w.astype(F32), axis=1, keepdims=True))
-                part.append(jnp.dot(w, vbuf[s, :, p].reshape(wide, hd), preferred_element_type=F32))
-                peak.append(m)
+            peak, total, part = ([d[p * slots + s] for s in range(slots)] for d in (peaks, totals, parts))
             lane_s = lax.broadcasted_iota(jnp.int32, (rows, hd), 1)
             tops = jnp.full((rows, hd), NEG, F32)
             sums = jnp.zeros((rows, hd), F32)
@@ -315,6 +329,42 @@
     st_recv[me] = st_send[last, mx // half, mz]
     rest_s = st_recv.at[pl.ds(0, n - 1)]
     rest_o = out_recv.at[pl.ds(0, n - 1)]
+    @pl.when(low & ~root)
+    def _():
+        pltpu.make_async_copy(two, two, x_send_sem).wait()
+
+    @pl.when(root | ~low)
+    def _():
+        pltpu.make_async_copy(three, three, x_send_sem).wait()
+
+    for z in range(nz):
+        @pl.when(~low & (z != mz) & (((z < mz) & ((mx > 0) | (z > 0))) | (z > mz)))
+        def _():
+            block_copy(mz, z, mx, block_send.at[z]).wait_send()
+
+        @pl.when(agent)
+        def _():
+            block_copy(z, 0, 0, root_send.at[z]).wait_send()
+
+        if z > 0:
+            @pl.when(low & ~root)
+            def _():
+                row_copy(first_row, z, mx, row_send.at[z], root_sem).wait_send()
+
+            @pl.when(agent)
+            def _():
+                row_copy(first_row, z, 0, row_send_low.at[z], root_sem).wait_send()
+
+            @pl.when(low & ~root)
+            def _():
+                block_copy(0, z, mx, block_send.at[z]).wait_send()
+
+            @pl.when(agent)
+            def _():
+                block_copy(0, z, 0, col_send.at[z]).wait_send()
+
+    pltpu.make_async_copy(rest_o, rest_o, o_send_sem).wait()
+    pltpu.make_async_copy(rest_s, rest_s, s_send_sem).wait()
     pltpu.make_async_copy(rest_s, rest_s, s_recv_sem).wait()
     pltpu.make_async_copy(rest_o, rest_o, o_recv_sem).wait()
 
@@ -332,43 +382,6 @@
         g = jnp.where(c == r, jnp.broadcast_to(f[i:i + 1], (group, hd)), 0.0)
         acc = acc + jnp.sum(g, axis=1, keepdims=True) * out_recv[i].astype(F32)
     o_ref[...] = acc.astype(BF16)
-
-    @pl.when(low & ~root)
-    def _():
-        pltpu.make_async_copy(two, two, x_send_sem).wait()
-
-    @pl.when(root | ~low)
-    def _():
-        pltpu.make_async_copy(three, three, x_send_sem).wait()
-
-    for z in range(nz):
-        @pl.when(~low & (z != mz) & (((z < mz) & ((mx > 0) | (z > 0))) | (z > mz)))
-        def _():
-            block_copy(mz, z, mx, block_send.at[z]).wait_send()
-
-        @pl.when(agent)
-        def _():
-            block_copy(z, 0, 0, root_send.at[z]).wait_send()
-
-        if z > 0:
-            @pl.when(low & ~root)
-            def _():
-                row_copy(first_row, z, mx, row_send.at[z], root_sem).wait_send()
-
-            @pl.when(agent)
-            def _():
-                row_copy(first_row, z, 0, row_send_low.at[z], root_sem).wait_send()
-
-            @pl.when(low & ~root)
-            def _():
-                block_copy(0, z, mx, block_send.at[z]).wait_send()
-
-            @pl.when(agent)
-            def _():
-                block_copy(0, z, 0, col_send.at[z]).wait_send()
-
-    pltpu.make_async_copy(rest_o, rest_o, o_send_sem).wait()
-    pltpu.make_async_copy(rest_s, rest_s, s_send_sem).wait()
 
 
 def solution(mesh):

time: 55.4 us -> 47.8 us (0.86)
  the two profiles are of different devices: /device:TPU:168 before, /device:TPU:40 now
where the time goes in v8:
time: 47.8 us; the launch traced here: 47.6 us
  Pallas kernels  46.4 us (97%)
  local copies, waits for them, and re-layouts  1.26 us (3%)
    pallas_call x1, Pallas kernels, body(): pl.pallas_call(functools.partial(attend, dims), out_shape=jax.ShapeDtypeS...  46.4 us
    unnamed x1, local copies, waits for them, and re-layouts  1.26 us

profile of v8, /device:TPU:40, one launch (start us, length us, event | category | flops | bytes accessed | tf_op | source)
XLA Modules:
  0.0 47.6 jit_solution(10415493705917399362)
XLA Ops:
  0.0 46.4 %shard_map.55 = bf16[8,128]{1,0:T(8,128)(2,1)} custom-call(bf16[8,128]{1,0:T(8,128)(2,1)} %bitcast.7, bf16[8,512,2,2,128]{4,3,2,1,0:T(2,128)(2,1)} %bitcast.4, bf16[8,512,2,2,128]{4,3,2,1,0:T(2,128)(2,1)} %bitcast.5, s32[16]{0:T(128)} %len_hbm.1, s32[8]{0:T(128)} %slot_hbm.1), custom_call_target="tpu_custom_call" | custom-call | tf_op jit(solution)/shard_map/pallas_call | solution.py:401
  46.4 1.3 %copy.7 = bf16[8,1,128]{2,0,1:T(8,128)(2,1)} copy(bf16[8,1,128]{2,0,1:T(8,128)(2,1)} %bitcast.6) | data formatting | bytes 4096

commit v9 on v8

--- a/solution.py
+++ b/solution.py
@@ -14,8 +14,8 @@
 NEG = -1e30
 
 
-def attend(dims, q_hbm, k_hbm, v_hbm, len_hbm, slot_hbm, o_ref,
-           kbuf, vbuf, ktr, gather, gather_stat, q_land, q_use, lens, slot, out_send, out_recv, st_send, st_recv,
+def attend(dims, q_hbm, k_hbm, v_hbm, len_hbm, slot_hbm, o_hbm,
+           kbuf, vbuf, ktr, gather, gather_stat, final, q_land, q_use, lens, slot, out_send, out_recv, st_send, st_recv,
            ksem, vsem, small_sem, ready, ready_low, x_ready, root_sem, row_send, row_send_low, root_send, col_send, x_send_sem, x_recv_sem, block_send, block_sem,
            o_send_sem, o_recv_sem, s_send_sem, s_recv_sem):
     nz, nx, slots, block, group, hd = dims
@@ -138,7 +138,21 @@
         def _():
             block_copy(mz, b, mx, block_send.at[b]).start()
 
+    def send_row(z):
+        @pl.when(low & ~root)
+        def _():
+            row_copy(first_row, z, mx, row_send.at[z], root_sem).start()
+
+        @pl.when(agent)
+        def _():
+            row_copy(first_row, z, 0, row_send_low.at[z], root_sem).start()
+
     for z in range(1, nz):
+        if z == middle:
+            @pl.when(low & ~root)
+            def _():
+                pltpu.make_async_copy(first_row, first_row, root_sem).wait()
+
         @pl.when((z > mz) & ~root)
         def _():
             pl.semaphore_wait(ready.at[z], 1)
@@ -156,18 +170,11 @@
             pl.semaphore_wait(ready_low.at[z], 1)
             block_copy(0, z, 0, col_send.at[z]).start()
 
-    @pl.when(low & ~root)
-    def _():
-        pltpu.make_async_copy(first_row, first_row, root_sem).wait()
-
-    for z in range(1, nz):
-        @pl.when(low & ~root)
-        def _():
-            row_copy(first_row, z, mx, row_send.at[z], root_sem).start()
-
-        @pl.when(agent)
-        def _():
-            row_copy(first_row, z, 0, row_send_low.at[z], root_sem).start()
+        if z >= middle:
+            send_row(z)
+
+    for z in range(1, middle):
+        send_row(z)
 
     @pl.when(agent)
     def _():
@@ -211,7 +218,7 @@
 
     def first(b):
         d = jnp.abs(mz - b)
-        near = (mz <= middle) | (b < reach) | (jnp.minimum(d, nz - d) <= reach + 1)
+        near = (mz <= middle) | (b <= reach) | (jnp.minimum(d, nz - d) <= reach + 1)
         return ((b <= mz) & (mz >= reach) & near).astype(jnp.int32)
 
     def goes(b, x, late):
@@ -381,7 +388,10 @@
     for i in range(n):
         g = jnp.where(c == r, jnp.broadcast_to(f[i:i + 1], (group, hd)), 0.0)
         acc = acc + jnp.sum(g, axis=1, keepdims=True) * out_recv[i].astype(F32)
-    o_ref[...] = acc.astype(BF16)
+    final[...] = acc.astype(BF16)
+    out = pltpu.make_async_copy(final, o_hbm, small_sem.at[2])
+    out.start()
+    out.wait()
 
 
 def solution(mesh):
@@ -402,12 +412,12 @@
             functools.partial(attend, dims),
             out_shape=jax.ShapeDtypeStruct((share, hd), BF16),
             in_specs=[any_] * 5,
-            out_specs=pl.BlockSpec(memory_space=pltpu.VMEM),
+            out_specs=any_,
             scratch_shapes=[
                 pltpu.VMEM(split, BF16), pltpu.VMEM(split, BF16),
                 pltpu.VMEM((slots, nx // half, hd, block * half), BF16),
                 pltpu.VMEM((nz * half * share, slots * half * share), BF16),
-                pltpu.VMEM((nz, hd), BF16),
+                pltpu.VMEM((nz, hd), BF16), pltpu.VMEM((share, hd), BF16),
                 pltpu.VMEM((nz, nx, share, hd), BF16), pltpu.VMEM((nz, nx, share, hd), BF16),
                 pltpu.SMEM((nz,), jnp.int32), pltpu.SMEM((slots,), jnp.int32),
                 pltpu.VMEM((2, nx, nz, share, hd), BF16), pltpu.VMEM((n, share, hd), BF16),

time: 47.8 us -> 47.8 us (level)
  no operation moved by 1% of the time
where the time goes in v9:
time: 47.8 us; the launch traced here: 47.7 us
  Pallas kernels  46.4 us (97%)
  local copies, waits for them, and re-layouts  1.26 us (3%)
    pallas_call x1, Pallas kernels, body(): pl.pallas_call(functools.partial(attend, dims), out_shape=jax.ShapeDtypeS...  46.4 us
    unnamed x1, local copies, waits for them, and re-layouts  1.26 us

profile of v9, /device:TPU:40, one launch (start us, length us, event | category | flops | bytes accessed | tf_op | source)
XLA Modules:
  0.0 47.7 jit_solution(1160543251467412231)
XLA Ops:
  0.0 46.4 %shard_map.55 = bf16[8,128]{1,0:T(8,128)(2,1)} custom-call(bf16[8,128]{1,0:T(8,128)(2,1)} %bitcast.7, bf16[8,512,2,2,128]{4,3,2,1,0:T(2,128)(2,1)} %bitcast.4, bf16[8,512,2,2,128]{4,3,2,1,0:T(2,128)(2,1)} %bitcast.5, s32[16]{0:T(128)} %len_hbm.1, s32[8]{0:T(128)} %slot_hbm.1), custom_call_target="tpu_custom_call" | custom-call | tf_op jit(solution)/shard_map/pallas_call | solution.py:411
  46.5 1.3 %copy.7 = bf16[8,1,128]{2,0,1:T(8,128)(2,1)} copy(bf16[8,1,128]{2,0,1:T(8,128)(2,1)} %bitcast.6) | data formatting | bytes 4096

commit v10 on v9

--- a/solution.py
+++ b/solution.py
@@ -16,7 +16,7 @@
 
 def attend(dims, q_hbm, k_hbm, v_hbm, len_hbm, slot_hbm, o_hbm,
            kbuf, vbuf, ktr, gather, gather_stat, final, q_land, q_use, lens, slot, out_send, out_recv, st_send, st_recv,
-           ksem, vsem, small_sem, ready, ready_low, x_ready, root_sem, row_send, row_send_low, root_send, col_send, x_send_sem, x_recv_sem, block_send, block_sem,
+           ksem, vsem, small_sem, ready, ready_low, x_ready, root_sem, row_send, root_send, col_send, x_send_sem, x_recv_sem, block_send, block_sem,
            o_send_sem, o_recv_sem, s_send_sem, s_recv_sem):
     nz, nx, slots, block, group, hd = dims
     n = nz * nx
@@ -86,8 +86,8 @@
         pltpu.make_async_copy(slot_hbm, slot, small_sem.at[0]),
         pltpu.make_async_copy(len_hbm, lens, small_sem.at[1]),
     ]
-    loads = [pltpu.make_async_copy(k_hbm.at[s], kbuf.at[s], ksem.at[s]) for s in range(slots)]
-    vloads = [pltpu.make_async_copy(v_hbm.at[s], vbuf.at[s], vsem.at[s]) for s in range(slots)]
+    loads = [pltpu.make_async_copy(k_hbm.at[s], kbuf.at[s], ksem) for s in range(slots)]
+    vloads = [pltpu.make_async_copy(v_hbm.at[s], vbuf.at[s], vsem) for s in range(slots)]
     for c in small + loads + vloads:
         c.start()
     own.wait()
@@ -136,16 +136,16 @@
     for b in range(top_z):
         @pl.when((b < mz) & ((mx > 0) | (b > 0)))
         def _():
-            block_copy(mz, b, mx, block_send.at[b]).start()
+            block_copy(mz, b, mx, block_send).start()
 
     def send_row(z):
         @pl.when(low & ~root)
         def _():
-            row_copy(first_row, z, mx, row_send.at[z], root_sem).start()
+            row_copy(first_row, z, mx, row_send, root_sem).start()
 
         @pl.when(agent)
         def _():
-            row_copy(first_row, z, 0, row_send_low.at[z], root_sem).start()
+            row_copy(first_row, z, 0, row_send, root_sem).start()
 
     for z in range(1, nz):
         if z == middle:
@@ -159,16 +159,16 @@
 
             @pl.when(~low)
             def _():
-                block_copy(mz, z, mx, block_send.at[z]).start()
+                block_copy(mz, z, mx, block_send).start()
 
             @pl.when(low)
             def _():
-                block_copy(0, z, mx, block_send.at[z]).start()
+                block_copy(0, z, mx, block_send).start()
 
         @pl.when(agent)
         def _():
             pl.semaphore_wait(ready_low.at[z], 1)
-            block_copy(0, z, 0, col_send.at[z]).start()
+            block_copy(0, z, 0, col_send).start()
 
         if z >= middle:
             send_row(z)
@@ -178,7 +178,7 @@
 
     @pl.when(agent)
     def _():
-        block_copy(0, 0, 0, root_send.at[0]).start()
+        block_copy(0, 0, 0, root_send).start()
 
     for c in small:
         c.wait()
@@ -207,18 +207,17 @@
     r = lax.broadcasted_iota(jnp.int32, (nz, hd), 0)
     gather_stat[...] = jnp.where(r == lane_seq, 1.0, 0.0).astype(BF16)
 
+    pltpu.make_async_copy(k_hbm, kbuf, ksem).wait()
     for s in range(slots):
-        loads[s].wait()
         for p in range(pairs):
             ktr[s, p] = kbuf[s, :, p].reshape(wide, hd).T
-    for s in range(slots):
-        vloads[s].wait()
+    pltpu.make_async_copy(v_hbm, vbuf, vsem).wait()
 
     row_pass = (mz < reach).astype(jnp.int32)
 
     def first(b):
         d = jnp.abs(mz - b)
-        near = (mz <= middle) | (b <= reach) | (jnp.minimum(d, nz - d) <= reach + 1)
+        near = (mz <= middle) | (b < reach) | (jnp.minimum(d, nz - d) <= reach + 1)
         return ((b <= mz) & (mz >= reach) & near).astype(jnp.int32)
 
     def goes(b, x, late):
@@ -235,7 +234,7 @@
             if b > 0:
                 @pl.when(agent)
                 def _():
-                    block_copy(b, 0, 0, root_send.at[b]).start()
+                    block_copy(b, 0, 0, root_send).start()
 
                 @pl.when((first(b) != late) & (b != mz))
                 def _():
@@ -344,31 +343,31 @@
     def _():
         pltpu.make_async_copy(three, three, x_send_sem).wait()
 
-    for z in range(nz):
-        @pl.when(~low & (z != mz) & (((z < mz) & ((mx > 0) | (z > 0))) | (z > mz)))
-        def _():
-            block_copy(mz, z, mx, block_send.at[z]).wait_send()
-
-        @pl.when(agent)
-        def _():
-            block_copy(z, 0, 0, root_send.at[z]).wait_send()
-
-        if z > 0:
-            @pl.when(low & ~root)
-            def _():
-                row_copy(first_row, z, mx, row_send.at[z], root_sem).wait_send()
-
-            @pl.when(agent)
-            def _():
-                row_copy(first_row, z, 0, row_send_low.at[z], root_sem).wait_send()
-
-            @pl.when(low & ~root)
-            def _():
-                block_copy(0, z, mx, block_send.at[z]).wait_send()
-
-            @pl.when(agent)
-            def _():
-                block_copy(0, z, 0, col_send.at[z]).wait_send()
+    def sent(sem, count):
+        moved = out_recv.at[pl.ds(0, count)]
+        pltpu.make_async_copy(moved, moved, sem).wait()
+
+    @pl.when(~low & (mx > 0))
+    def _():
+        sent(block_send, (nz - 1) * nx)
+
+    @pl.when(~low & (mx == 0))
+    def _():
+        sent(block_send, (nz - 2) * nx)
+
+    @pl.when(low & ~root)
+    def _():
+        sent(block_send, (nz - 1) * (nx - 1))
+
+    @pl.when(low & ~root & ~agent)
+    def _():
+        sent(row_send, nz - 1)
+
+    @pl.when(agent)
+    def _():
+        sent(row_send, 2 * (nz - 1))
+        sent(col_send, (nz - 1) * (nx - 1))
+        sent(root_send, n - 1)
 
     pltpu.make_async_copy(rest_o, rest_o, o_send_sem).wait()
     pltpu.make_async_copy(rest_s, rest_s, s_send_sem).wait()
@@ -422,8 +421,8 @@
                 pltpu.SMEM((nz,), jnp.int32), pltpu.SMEM((slots,), jnp.int32),
                 pltpu.VMEM((2, nx, nz, share, hd), BF16), pltpu.VMEM((n, share, hd), BF16),
                 pltpu.VMEM((2, nx // half, nz, 1, hd), F32), pltpu.VMEM((n, 1, hd), F32),
-                dma((slots,)), dma((slots,)), dma((3,)), regular((nz,)), regular((nz,)), regular((nx,)), dma, dma((nz,)), dma((nz,)), dma((nz,)), dma((nz,)), dma, dma,
-                dma((nz,)), dma((nz,)), dma, dma, dma, dma,
+                dma, dma, dma((3,)), regular((nz,)), regular((nz,)), regular((nx,)), dma, dma, dma, dma,
+                dma, dma, dma, dma((nz,)), dma, dma, dma, dma,
             ],
             compiler_params=pltpu.CompilerParams(collective_id=0, has_side_effects=True),
         )(queries.reshape(share, hd), keys.reshape(split), values.reshape(split), lengths, slot_block)

time: 47.8 us -> 45.7 us (0.956)
  Pallas kernels: 46.4 us -> 44.3 us
    pallas_call x1, Pallas kernels: 46.4 us -> 44.3 us  [body(): pl.pallas_call(functools.partial(attend, dims), out_shape=jax.ShapeDtypeS...]
where the time goes in v10:
time: 45.7 us; the launch traced here: 45.6 us
  Pallas kernels  44.3 us (97%)
  local copies, waits for them, and re-layouts  1.26 us (3%)
    pallas_call x1, Pallas kernels, body(): pl.pallas_call(functools.partial(attend, dims), out_shape=jax.ShapeDtypeS...  44.3 us
    unnamed x1, local copies, waits for them, and re-layouts  1.26 us

profile of v10, /device:TPU:40, one launch (start us, length us, event | category | flops | bytes accessed | tf_op | source)
XLA Modules:
  0.0 45.6 jit_solution(8585340278891109215)
XLA Ops:
  0.0 44.3 %shard_map.55 = bf16[8,128]{1,0:T(8,128)(2,1)} custom-call(bf16[8,128]{1,0:T(8,128)(2,1)} %bitcast.7, bf16[8,512,2,2,128]{4,3,2,1,0:T(2,128)(2,1)} %bitcast.4, bf16[8,512,2,2,128]{4,3,2,1,0:T(2,128)(2,1)} %bitcast.5, s32[16]{0:T(128)} %len_hbm.1, s32[8]{0:T(128)} %slot_hbm.1), custom_call_target="tpu_custom_call" | custom-call | tf_op jit(solution)/shard_map/pallas_call | solution.py:410
  44.3 1.3 %copy.7 = bf16[8,1,128]{2,0,1:T(8,128)(2,1)} copy(bf16[8,1,128]{2,0,1:T(8,128)(2,1)} %bitcast.6) | data formatting | bytes 4096

commit v11 on v10

--- a/solution.py
+++ b/solution.py
@@ -16,7 +16,7 @@
 
 def attend(dims, q_hbm, k_hbm, v_hbm, len_hbm, slot_hbm, o_hbm,
            kbuf, vbuf, ktr, gather, gather_stat, final, q_land, q_use, lens, slot, out_send, out_recv, st_send, st_recv,
-           ksem, vsem, small_sem, ready, ready_low, x_ready, root_sem, row_send, root_send, col_send, x_send_sem, x_recv_sem, block_send, block_sem,
+           ksem, vsem, small_sem, ready, x_ready, root_sem, row_send, root_send, col_send, x_send_sem, x_recv_sem, block_send, block_sem,
            o_send_sem, o_recv_sem, s_send_sem, s_recv_sem):
     nz, nx, slots, block, group, hd = dims
     n = nz * nx
@@ -75,7 +75,7 @@
 
     @pl.when((mx == 0) & ~low)
     def _():
-        pl.semaphore_signal(ready_low.at[mz], inc=1, device_id=at(0, 1), device_id_type=MESH)
+        pl.semaphore_signal(ready.at[mz], inc=1, device_id=at(0, 1), device_id_type=MESH)
 
     for x in range(nx - 1):
         @pl.when((x < mx) & ((x > 0) | ~low))
@@ -155,7 +155,7 @@
 
         @pl.when((z > mz) & ~root)
         def _():
-            pl.semaphore_wait(ready.at[z], 1)
+            pl.semaphore_wait(ready.at[z], 1 + agent.astype(jnp.int32))
 
             @pl.when(~low)
             def _():
@@ -167,7 +167,6 @@
 
         @pl.when(agent)
         def _():
-            pl.semaphore_wait(ready_low.at[z], 1)
             block_copy(0, z, 0, col_send).start()
 
         if z >= middle:
@@ -220,8 +219,11 @@
         near = (mz <= middle) | (b < reach) | (jnp.minimum(d, nz - d) <= reach + 1)
         return ((b <= mz) & (mz >= reach) & near).astype(jnp.int32)
 
+    def made(b, x):
+        return row_pass if b == 0 and x == 0 else 1 - first(b)
+
     def goes(b, x, late):
-        return late == row_pass if b == 0 and x == 0 else first(b) != late
+        return late == (made(b, x) if b < reach else jnp.where(mz >= middle, 1, made(b, x)))
 
     scale = hd ** -0.5 * math.log2(math.e)
 
@@ -320,11 +322,11 @@
                 @pl.when(goes(b, x, late) & (b * nx + x != me))
                 def _():
                     pltpu.make_async_remote_copy(
-                        src_ref=out_send.at[late, x, b], dst_ref=out_recv.at[me],
+                        src_ref=out_send.at[made(b, x), x, b], dst_ref=out_recv.at[me],
                         send_sem=o_send_sem, recv_sem=o_recv_sem,
                         device_id=at(b, x), device_id_type=MESH).start()
                     pltpu.make_async_remote_copy(
-                        src_ref=st_send.at[late, x // half, b], dst_ref=st_recv.at[me],
+                        src_ref=st_send.at[made(b, x), x // half, b], dst_ref=st_recv.at[me],
                         send_sem=s_send_sem, recv_sem=s_recv_sem,
                         device_id=at(b, x), device_id_type=MESH).start()
         return carry
@@ -421,7 +423,7 @@
                 pltpu.SMEM((nz,), jnp.int32), pltpu.SMEM((slots,), jnp.int32),
                 pltpu.VMEM((2, nx, nz, share, hd), BF16), pltpu.VMEM((n, share, hd), BF16),
                 pltpu.VMEM((2, nx // half, nz, 1, hd), F32), pltpu.VMEM((n, 1, hd), F32),
-                dma, dma, dma((3,)), regular((nz,)), regular((nz,)), regular((nx,)), dma, dma, dma, dma,
+                dma, dma, dma((3,)), regular((nz,)), regular((nx,)), dma, dma, dma, dma,
                 dma, dma, dma, dma((nz,)), dma, dma, dma, dma,
             ],
             compiler_params=pltpu.CompilerParams(collective_id=0, has_side_effects=True),

time: 45.7 us -> 45.7 us (level)
  no operation moved by 1% of the time
where the time goes in v11:
time: 45.7 us; the launch traced here: 45.5 us
  Pallas kernels  44.3 us (97%)
  local copies, waits for them, and re-layouts  1.26 us (3%)
    pallas_call x1, Pallas kernels, body(): pl.pallas_call(functools.partial(attend, dims), out_shape=jax.ShapeDtypeS...  44.3 us
    unnamed x1, local copies, waits for them, and re-layouts  1.26 us

profile of v11, /device:TPU:40, one launch (start us, length us, event | category | flops | bytes accessed | tf_op | source)
XLA Modules:
  0.0 45.5 jit_solution(16278745823963020969)
XLA Ops:
  0.0 44.3 %shard_map.55 = bf16[8,128]{1,0:T(8,128)(2,1)} custom-call(bf16[8,128]{1,0:T(8,128)(2,1)} %bitcast.7, bf16[8,512,2,2,128]{4,3,2,1,0:T(2,128)(2,1)} %bitcast.4, bf16[8,512,2,2,128]{4,3,2,1,0:T(2,128)(2,1)} %bitcast.5, s32[16]{0:T(128)} %len_hbm.1, s32[8]{0:T(128)} %slot_hbm.1), custom_call_target="tpu_custom_call" | custom-call | tf_op jit(solution)/shard_map/pallas_call | solution.py:412
  44.3 1.3 %copy.7 = bf16[8,1,128]{2,0,1:T(8,128)(2,1)} copy(bf16[8,1,128]{2,0,1:T(8,128)(2,1)} %bitcast.6) | data formatting | bytes 4096

commit v12 on v11

--- a/solution.py
+++ b/solution.py
@@ -219,11 +219,8 @@
         near = (mz <= middle) | (b < reach) | (jnp.minimum(d, nz - d) <= reach + 1)
         return ((b <= mz) & (mz >= reach) & near).astype(jnp.int32)
 
-    def made(b, x):
-        return row_pass if b == 0 and x == 0 else 1 - first(b)
-
     def goes(b, x, late):
-        return late == (made(b, x) if b < reach else jnp.where(mz >= middle, 1, made(b, x)))
+        return late == row_pass if b == 0 and x == 0 else first(b) != late
 
     scale = hd ** -0.5 * math.log2(math.e)
 
@@ -322,11 +319,11 @@
                 @pl.when(goes(b, x, late) & (b * nx + x != me))
                 def _():
                     pltpu.make_async_remote_copy(
-                        src_ref=out_send.at[made(b, x), x, b], dst_ref=out_recv.at[me],
+                        src_ref=out_send.at[late, x, b], dst_ref=out_recv.at[me],
                         send_sem=o_send_sem, recv_sem=o_recv_sem,
                         device_id=at(b, x), device_id_type=MESH).start()
                     pltpu.make_async_remote_copy(
-                        src_ref=st_send.at[made(b, x), x // half, b], dst_ref=st_recv.at[me],
+                        src_ref=st_send.at[late, x // half, b], dst_ref=st_recv.at[me],
                         send_sem=s_send_sem, recv_sem=s_recv_sem,
                         device_id=at(b, x), device_id_type=MESH).start()
         return carry

time: 45.7 us -> 45.6 us (level)
  no operation moved by 1% of the time
where the time goes in v12:
time: 45.6 us; the launch traced here: 45.4 us
  Pallas kernels  44.2 us (97%)
  local copies, waits for them, and re-layouts  1.26 us (3%)
    pallas_call x1, Pallas kernels, body(): pl.pallas_call(functools.partial(attend, dims), out_shape=jax.ShapeDtypeS...  44.2 us
    unnamed x1, local copies, waits for them, and re-layouts  1.26 us

profile of v12, /device:TPU:40, one launch (start us, length us, event | category | flops | bytes accessed | tf_op | source)
XLA Modules:
  0.0 45.4 jit_solution(3889859652166274118)
XLA Ops:
  0.0 44.2 %shard_map.55 = bf16[8,128]{1,0:T(8,128)(2,1)} custom-call(bf16[8,128]{1,0:T(8,128)(2,1)} %bitcast.7, bf16[8,512,2,2,128]{4,3,2,1,0:T(2,128)(2,1)} %bitcast.4, bf16[8,512,2,2,128]{4,3,2,1,0:T(2,128)(2,1)} %bitcast.5, s32[16]{0:T(128)} %len_hbm.1, s32[8]{0:T(128)} %slot_hbm.1), custom_call_target="tpu_custom_call" | custom-call | tf_op jit(solution)/shard_map/pallas_call | solution.py:409
  44.2 1.3 %copy.7 = bf16[8,1,128]{2,0,1:T(8,128)(2,1)} copy(bf16[8,1,128]{2,0,1:T(8,128)(2,1)} %bitcast.6) | data formatting | bytes 4096
